TPU v7x, 128 devices: a whole 4x4x4 slice. The times are simulated.
128 devices in a mesh: dp: 1, tp: 16 (over z, y), pp: 8 (over x, core).
Axes of the slice: x: 4, y: 4, z: 4, core: 2. Of those that a mesh axis runs over, the one named last changes fastest.
Arguments:
- tokens: int32 [32, 64], P('dp')
- labels: int32 [32, 64], P('dp')
- emb_table: bfloat16 [50304, 1024], P('tp')
- w_in: bfloat16 [8, 1024, 4096], P('pp', None, 'tp')
- w_out: bfloat16 [8, 4096, 1024], P('pp', 'tp')
Outputs:
- output 1: float32 [1], P('dp')
- output 2: float32 [8, 1024, 4096], P(('dp', 'pp'), None, 'tp')
- output 3: float32 [8, 4096, 1024], P(('dp', 'pp'), 'tp')
- output 4: float32 [50304, 1024], P(('dp', 'tp'))
All inputs are finite; a program needn't handle non-finite values.
Results may differ from a plain program's by a relative error of at most 0.012808.
Values are sent between devices in bfloat16 or wider.
A program may use at most 1 GiB of HBM per device.

v0:
```python
import jax
import jax.numpy as jnp
from jax import lax
from jax.sharding import PartitionSpec as P

NORM_EPS = 1e-6


def contract(lhs, rhs, lhs_dim, rhs_dim):
    return lax.dot_general(lhs, rhs, (((lhs_dim,), (rhs_dim,)), ((), ())), preferred_element_type=jnp.float32)


def solution(mesh):
    pp_size = mesh.shape['pp']
    fwd_perm = [(src_stage, src_stage + 1) for src_stage in range(pp_size - 1)]
    bwd_perm = [(src_stage + 1, src_stage) for src_stage in range(pp_size - 1)]

    def device_fn(tokens, labels, emb_table, w_in, w_out):
        num_micro, seq_len = tokens.shape
        vocab_rows, model_dim = emb_table.shape
        w_one = w_in[0]
        w_two = w_out[0]
        hidden_cols = w_one.shape[1]
        stage_idx = lax.axis_index('pp')
        is_first = stage_idx == 0
        is_last = stage_idx == pp_size - 1
        vocab_base = lax.axis_index('tp') * vocab_rows
        tok_local = tokens - vocab_base
        lab_local = labels - vocab_base
        row_ids = jnp.arange(vocab_rows, dtype=jnp.int32)
        num_ticks = num_micro + pp_size - 1
        act_zero = jnp.zeros((seq_len, model_dim), jnp.bfloat16)

        owned_ids = (tok_local >= 0) & (tok_local < vocab_rows) & is_first
        looked_up = jnp.take(emb_table, jnp.clip(tok_local, 0, vocab_rows - 1), axis=0)
        x_first = lax.psum(jnp.where(owned_ids[:, :, None], looked_up, jnp.zeros_like(looked_up)), 'tp')

        def fwd_tick(x_recv, tick_idx):
            fresh_in = lax.dynamic_index_in_dim(x_first, jnp.minimum(tick_idx, num_micro - 1), 0, keepdims=False)
            x_act = jnp.where(is_first, fresh_in, x_recv)
            hidden = jnp.dot(x_act, w_one, preferred_element_type=jnp.float32)
            gate_act = jax.nn.gelu(hidden).astype(jnp.bfloat16)
            branch_out = lax.psum(jnp.dot(gate_act, w_two, preferred_element_type=jnp.float32), 'tp')
            y_act = (x_act.astype(jnp.float32) + branch_out).astype(jnp.bfloat16)
            return lax.ppermute(y_act, 'pp', fwd_perm), (x_act, hidden, y_act)

        x_hist, h_hist, y_hist = lax.scan(fwd_tick, act_zero, jnp.arange(num_ticks))[1]
        x_saved = lax.dynamic_slice_in_dim(x_hist, stage_idx, num_micro, 0)
        h_saved = lax.dynamic_slice_in_dim(h_hist, stage_idx, num_micro, 0)
        y_top = y_hist[pp_size - 1:]

        def head_step(carry_in, micro_in):
            loss_sum, head_grad = carry_in
            y_act, lab_row = micro_in
            x_wide = y_act.astype(jnp.float32)
            inv_rms = lax.rsqrt(jnp.mean(x_wide * x_wide, axis=-1, keepdims=True) + NORM_EPS)
            normed = x_wide * inv_rms
            normed_b = normed.astype(jnp.bfloat16)
            target_hit = lab_row[:, None] == row_ids[None, :]

            def logit_part():
                logits = contract(normed_b, emb_table, 1, 1)
                local_lse = jax.nn.logsumexp(logits, axis=-1)
                local_target = jnp.sum(jnp.where(target_hit, logits, 0.0), axis=-1)
                return logits, local_lse, local_target

            def logit_skip():
                flat_zero = jnp.zeros((seq_len,), jnp.float32)
                return jnp.zeros((seq_len, vocab_rows), jnp.float32), flat_zero, flat_zero

            logits, local_lse, local_target = lax.cond(is_last, logit_part, logit_skip)
            log_norm = jax.nn.logsumexp(lax.all_gather(local_lse, 'tp'), axis=0)
            target_logit = lax.psum(local_target, 'tp')

            def grad_part():
                grad_logits = (jnp.exp(logits - log_norm[:, None]) - target_hit.astype(jnp.float32)).astype(jnp.bfloat16)
                return head_grad + contract(grad_logits, normed_b, 0, 0), contract(grad_logits, emb_table, 1, 0)

            def grad_skip():
                return head_grad, jnp.zeros((seq_len, model_dim), jnp.float32)

            new_head, normed_part = lax.cond(is_last, grad_part, grad_skip)
            grad_normed = lax.psum(normed_part, 'tp')
            grad_top = (inv_rms * (grad_normed - normed * jnp.mean(normed * grad_normed, axis=-1, keepdims=True))).astype(jnp.bfloat16)
            return (loss_sum + jnp.sum(log_norm - target_logit), new_head), grad_top

        head_init = (jnp.zeros((), jnp.float32), jnp.zeros((vocab_rows, model_dim), jnp.float32))
        head_out, grad_tops = lax.scan(head_step, head_init, (y_top, lab_local))
        loss_sum, head_grad = head_out

        def bwd_tick(carry_in, tick_idx):
            g_recv, acc_one, acc_two, acc_table = carry_in
            micro_idx = tick_idx - (pp_size - 1 - stage_idx)
            is_valid = (micro_idx >= 0) & (micro_idx < num_micro)
            pick_idx = jnp.clip(micro_idx, 0, num_micro - 1)
            top_in = lax.dynamic_index_in_dim(grad_tops, pick_idx, 0, keepdims=False)
            grad_y = jnp.where(is_valid, jnp.where(is_last, top_in, g_recv), act_zero)
            x_act = lax.dynamic_index_in_dim(x_saved, pick_idx, 0, keepdims=False)
            hidden = lax.dynamic_index_in_dim(h_saved, pick_idx, 0, keepdims=False)
            gate_act, gelu_vjp = jax.vjp(jax.nn.gelu, hidden)
            grad_hidden = gelu_vjp(contract(grad_y, w_two, 1, 1))[0].astype(jnp.bfloat16)
            acc_two = acc_two + contract(gate_act.astype(jnp.bfloat16), grad_y, 0, 0)
            acc_one = acc_one + contract(x_act, grad_hidden, 0, 0)
            grad_x = (grad_y.astype(jnp.float32) + lax.psum(contract(grad_hidden, w_one, 1, 1), 'tp')).astype(jnp.bfloat16)
            tok_row = lax.dynamic_index_in_dim(tok_local, pick_idx, 0, keepdims=False)

            def add_rows():
                one_hot = (tok_row[:, None] == row_ids[None, :]).astype(jnp.bfloat16)
                return acc_table + contract(one_hot, grad_x, 0, 0)

            def keep_rows():
                return acc_table

            new_table = lax.cond(is_first, add_rows, keep_rows)
            return (lax.ppermute(grad_x, 'pp', bwd_perm), acc_one, acc_two, new_table), None

        bwd_init = (act_zero, jnp.zeros((model_dim, hidden_cols), jnp.float32), jnp.zeros((hidden_cols, model_dim), jnp.float32), jnp.zeros((vocab_rows, model_dim), jnp.float32))
        bwd_out = lax.scan(bwd_tick, bwd_init, jnp.arange(num_ticks))[0]
        grad_table = lax.psum(bwd_out[3] + head_grad, 'pp')
        mean_loss = lax.psum(jnp.where(is_last, loss_sum, 0.0), 'pp') / (num_micro * seq_len)
        return mean_loss.reshape(1), bwd_out[1][None], bwd_out[2][None], grad_table

    return jax.shard_map(device_fn, mesh=mesh, in_specs=(P('dp', None), P('dp', None), P('tp', None), P('pp', None, 'tp'), P('pp', 'tp', None)), out_specs=(P('dp'), P(('dp', 'pp'), None, 'tp'), P(('dp', 'pp'), 'tp', None), P(('dp', 'tp'), None)), check_vma=False)
```

profile of v0, /device:TPU:1, one launch (start us, length us, event | category | flops | bytes accessed | tf_op | source)
XLA Modules:
  0.0 12690.1 jit_solution(1375452190706437044)
XLA Ops:
  27.5 105.7 all-reduce.12.cloned.1.call-done
  133.8 3800.0 %while.59 = (s32[]{:T(128)}, bf16[64,1024]{1,0:T(8,128)(2,1)S(1)}, bf16[39,64,1024]{2,1,0:T(8,128)(2,1)}, f32[39,64,256]{2,1,0:T(8,128)}, bf16[39,64,1024]{2,1,0...) while((s32[]{:T(128)}, bf16[64,1024]{1,0:T(8,128)(2,1)S(1)}, ...), condition=%wide.region_3.4_spmd.clone, body=%wide.region_1.3_spmd.sunk.clone | while | flops 67584000 | bytes 4917499 | solution.py:47
  3950.9 4574.7 %while.60 = (s32[]{:T(128)}, f32[]{:T(128)}, f32[3144,1024]{1,0:T(8,128)}, bf16[32,64,1024]{2,1,0:T(8,128)(2,1)}, pred[]{:T(512)}, /*index=5*/bf16[32,64,1024]{2...) while((s32[]{:T(128)}, f32[]{:T(128)}, ...), condition=%wide.region_19.20_spmd.clone.clone, body=%wide.region_4.19_spmd.clone.sunk.clone | while | flops 1243426560 | bytes 47152772 | solution.py:88
  4130.3 101.2 all-reduce.18.cloned.1.call-done
  4273.3 101.2 all-reduce.18.cloned.1.call-done
  4416.3 101.2 all-reduce.18.cloned.1.call-done
  4559.3 101.2 all-reduce.18.cloned.1.call-done
  4702.4 101.3 all-reduce.18.cloned.1.call-done
  4845.4 101.3 all-reduce.18.cloned.1.call-done
  5274.5 101.2 all-reduce.18.cloned.1.call-done
  5417.5 101.3 all-reduce.18.cloned.1.call-done
  5560.6 101.2 all-reduce.18.cloned.1.call-done
  5703.6 101.2 all-reduce.18.cloned.1.call-done
  5989.7 101.2 all-reduce.18.cloned.1.call-done
  6132.7 101.3 all-reduce.18.cloned.1.call-done
  6275.8 101.2 all-reduce.18.cloned.1.call-done
  6418.8 101.2 all-reduce.18.cloned.1.call-done
  6561.8 101.3 all-reduce.18.cloned.1.call-done
  6704.8 101.3 all-reduce.18.cloned.1.call-done
  6847.9 101.2 all-reduce.18.cloned.1.call-done
  6990.9 101.2 all-reduce.18.cloned.1.call-done
  7134.0 101.3 all-reduce.18.cloned.1.call-done
  7277.0 101.2 all-reduce.18.cloned.1.call-done
  7420.1 101.2 all-reduce.18.cloned.1.call-done
  7563.1 101.3 all-reduce.18.cloned.1.call-done
  7706.2 101.3 all-reduce.18.cloned.1.call-done
  7849.3 101.3 all-reduce.18.cloned.1.call-done
  7992.3 101.3 all-reduce.18.cloned.1.call-done
  8135.4 101.2 all-reduce.18.cloned.1.call-done
  8278.4 101.2 all-reduce.18.cloned.1.call-done
  8531.9 3971.1 %while.61 = (s32[]{:T(128)}, bf16[64,1024]{1,0:T(8,128)(2,1)S(1)}, f32[1024,256]{1,0:T(8,128)S(1)}, f32[256,1024]{1,0:T(8,128)S(1)}, f32[3144,1024]{1,0:T(8,128)...) while((s32[]{:T(128)}, bf16[64,1024]{1,0:T(8,128)(2,1)S(1)}, ...), condition=%wide.region_25.26_spmd.clone.clone, body=%wide.region_21.25_spmd.clone.sunk.clone | while | flops 551645696 | bytes 35056304 | solution.py:118
  12540.4 129.4 %all-reduce.14.cloned.1.call-done = f32[3144,1024]{1,0:T(8,128)} async-done(((f32[3144,1024]{1,0:T(8,128)}), f32[3144,1024]{1,0:T(8,128)}) %all-reduce.14.cloned.1.call-update) | async-done | bytes 12877840 | tf_op jit(solution)/shard_map/psum | solution.py:119
  (1854 shorter events, 9638.4 us)
Async XLA Ops:
  4091.4 140.1 %all-reduce.18.cloned.1.call-start = ((), (), s32[]{:S(2)}) async-start(), calls=%async_computation.3 | async-start | bytes 524288 | tf_op jit(solution)/shard_map/while/body/eval_jaxpr/psum | solution.py:83
  4234.5 140.1 %all-reduce.18.cloned.1.call-start = ((), (), s32[]{:S(2)}) async-start(), calls=%async_computation.3 | async-start | bytes 524288 | tf_op jit(solution)/shard_map/while/body/eval_jaxpr/psum | solution.py:83
  4377.5 140.1 %all-reduce.18.cloned.1.call-start = ((), (), s32[]{:S(2)}) async-start(), calls=%async_computation.3 | async-start | bytes 524288 | tf_op jit(solution)/shard_map/while/body/eval_jaxpr/psum | solution.py:83
  4520.5 140.1 %all-reduce.18.cloned.1.call-start = ((), (), s32[]{:S(2)}) async-start(), calls=%async_computation.3 | async-start | bytes 524288 | tf_op jit(solution)/shard_map/while/body/eval_jaxpr/psum | solution.py:83
  4663.5 140.1 %all-reduce.18.cloned.1.call-start = ((), (), s32[]{:S(2)}) async-start(), calls=%async_computation.3 | async-start | bytes 524288 | tf_op jit(solution)/shard_map/while/body/eval_jaxpr/psum | solution.py:83
  4806.6 140.1 %all-reduce.18.cloned.1.call-start = ((), (), s32[]{:S(2)}) async-start(), calls=%async_computation.3 | async-start | bytes 524288 | tf_op jit(solution)/shard_map/while/body/eval_jaxpr/psum | solution.py:83
  4949.6 140.1 %all-reduce.18.cloned.1.call-start = ((), (), s32[]{:S(2)}) async-start(), calls=%async_computation.3 | async-start | bytes 524288 | tf_op jit(solution)/shard_map/while/body/eval_jaxpr/psum | solution.py:83
  5092.6 140.1 %all-reduce.18.cloned.1.call-start = ((), (), s32[]{:S(2)}) async-start(), calls=%async_computation.3 | async-start | bytes 524288 | tf_op jit(solution)/shard_map/while/body/eval_jaxpr/psum | solution.py:83
  5235.7 140.1 %all-reduce.18.cloned.1.call-start = ((), (), s32[]{:S(2)}) async-start(), calls=%async_computation.3 | async-start | bytes 524288 | tf_op jit(solution)/shard_map/while/body/eval_jaxpr/psum | solution.py:83
  5378.7 140.1 %all-reduce.18.cloned.1.call-start = ((), (), s32[]{:S(2)}) async-start(), calls=%async_computation.3 | async-start | bytes 524288 | tf_op jit(solution)/shard_map/while/body/eval_jaxpr/psum | solution.py:83
  5521.8 140.1 %all-reduce.18.cloned.1.call-start = ((), (), s32[]{:S(2)}) async-start(), calls=%async_computation.3 | async-start | bytes 524288 | tf_op jit(solution)/shard_map/while/body/eval_jaxpr/psum | solution.py:83
  5664.8 140.1 %all-reduce.18.cloned.1.call-start = ((), (), s32[]{:S(2)}) async-start(), calls=%async_computation.3 | async-start | bytes 524288 | tf_op jit(solution)/shard_map/while/body/eval_jaxpr/psum | solution.py:83
  5807.8 140.1 %all-reduce.18.cloned.1.call-start = ((), (), s32[]{:S(2)}) async-start(), calls=%async_computation.3 | async-start | bytes 524288 | tf_op jit(solution)/shard_map/while/body/eval_jaxpr/psum | solution.py:83
  5950.8 140.1 %all-reduce.18.cloned.1.call-start = ((), (), s32[]{:S(2)}) async-start(), calls=%async_computation.3 | async-start | bytes 524288 | tf_op jit(solution)/shard_map/while/body/eval_jaxpr/psum | solution.py:83
  6093.9 140.1 %all-reduce.18.cloned.1.call-start = ((), (), s32[]{:S(2)}) async-start(), calls=%async_computation.3 | async-start | bytes 524288 | tf_op jit(solution)/shard_map/while/body/eval_jaxpr/psum | solution.py:83
  6236.9 140.1 %all-reduce.18.cloned.1.call-start = ((), (), s32[]{:S(2)}) async-start(), calls=%async_computation.3 | async-start | bytes 524288 | tf_op jit(solution)/shard_map/while/body/eval_jaxpr/psum | solution.py:83
  6379.9 140.1 %all-reduce.18.cloned.1.call-start = ((), (), s32[]{:S(2)}) async-start(), calls=%async_computation.3 | async-start | bytes 524288 | tf_op jit(solution)/shard_map/while/body/eval_jaxpr/psum | solution.py:83
  6522.9 140.1 %all-reduce.18.cloned.1.call-start = ((), (), s32[]{:S(2)}) async-start(), calls=%async_computation.3 | async-start | bytes 524288 | tf_op jit(solution)/shard_map/while/body/eval_jaxpr/psum | solution.py:83
  6666.0 140.1 %all-reduce.18.cloned.1.call-start = ((), (), s32[]{:S(2)}) async-start(), calls=%async_computation.3 | async-start | bytes 524288 | tf_op jit(solution)/shard_map/while/body/eval_jaxpr/psum | solution.py:83
  6809.1 140.1 %all-reduce.18.cloned.1.call-start = ((), (), s32[]{:S(2)}) async-start(), calls=%async_computation.3 | async-start | bytes 524288 | tf_op jit(solution)/shard_map/while/body/eval_jaxpr/psum | solution.py:83
  6952.1 140.1 %all-reduce.18.cloned.1.call-start = ((), (), s32[]{:S(2)}) async-start(), calls=%async_computation.3 | async-start | bytes 524288 | tf_op jit(solution)/shard_map/while/body/eval_jaxpr/psum | solution.py:83
  7095.1 140.1 %all-reduce.18.cloned.1.call-start = ((), (), s32[]{:S(2)}) async-start(), calls=%async_computation.3 | async-start | bytes 524288 | tf_op jit(solution)/shard_map/while/body/eval_jaxpr/psum | solution.py:83
  7238.2 140.1 %all-reduce.18.cloned.1.call-start = ((), (), s32[]{:S(2)}) async-start(), calls=%async_computation.3 | async-start | bytes 524288 | tf_op jit(solution)/shard_map/while/body/eval_jaxpr/psum | solution.py:83
  7381.2 140.1 %all-reduce.18.cloned.1.call-start = ((), (), s32[]{:S(2)}) async-start(), calls=%async_computation.3 | async-start | bytes 524288 | tf_op jit(solution)/shard_map/while/body/eval_jaxpr/psum | solution.py:83
  7524.3 140.1 %all-reduce.18.cloned.1.call-start = ((), (), s32[]{:S(2)}) async-start(), calls=%async_computation.3 | async-start | bytes 524288 | tf_op jit(solution)/shard_map/while/body/eval_jaxpr/psum | solution.py:83
  7667.3 140.1 %all-reduce.18.cloned.1.call-start = ((), (), s32[]{:S(2)}) async-start(), calls=%async_computation.3 | async-start | bytes 524288 | tf_op jit(solution)/shard_map/while/body/eval_jaxpr/psum | solution.py:83
  7810.4 140.1 %all-reduce.18.cloned.1.call-start = ((), (), s32[]{:S(2)}) async-start(), calls=%async_computation.3 | async-start | bytes 524288 | tf_op jit(solution)/shard_map/while/body/eval_jaxpr/psum | solution.py:83
  7953.5 140.1 %all-reduce.18.cloned.1.call-start = ((), (), s32[]{:S(2)}) async-start(), calls=%async_computation.3 | async-start | bytes 524288 | tf_op jit(solution)/shard_map/while/body/eval_jaxpr/psum | solution.py:83
  8096.5 140.1 %all-reduce.18.cloned.1.call-start = ((), (), s32[]{:S(2)}) async-start(), calls=%async_computation.3 | async-start | bytes 524288 | tf_op jit(solution)/shard_map/while/body/eval_jaxpr/psum | solution.py:83
  8239.6 140.1 %all-reduce.18.cloned.1.call-start = ((), (), s32[]{:S(2)}) async-start(), calls=%async_computation.3 | async-start | bytes 524288 | tf_op jit(solution)/shard_map/while/body/eval_jaxpr/psum | solution.py:83
  8382.6 140.1 %all-reduce.18.cloned.1.call-start = ((), (), s32[]{:S(2)}) async-start(), calls=%async_computation.3 | async-start | bytes 524288 | tf_op jit(solution)/shard_map/while/body/eval_jaxpr/psum | solution.py:83
  12502.9 166.9 %all-reduce.14.cloned.1.call-start = ((), (), s32[]{:S(2)}) async-start(), calls=%async_computation.1 | async-start | bytes 25755648 | tf_op jit(solution)/shard_map/psum | solution.py:119
  (199 other events, 8214.1 us)
Sparse Core Ops, SparseCore 0:
  26.9 106.2 all-reduce.11
  4129.8 101.6 all-reduce.17
  4272.8 101.6 all-reduce.17
  4415.8 101.6 all-reduce.17
  4558.8 101.6 all-reduce.17
  4701.9 101.7 all-reduce.17
  4844.9 101.7 all-reduce.17
  4988.0 101.6 all-reduce.17
  5131.0 101.6 all-reduce.17
  5274.0 101.6 all-reduce.17
  5417.0 101.7 all-reduce.17
  5560.1 101.6 all-reduce.17
  5703.1 101.6 all-reduce.17
  5846.2 101.6 all-reduce.17
  5989.2 101.6 all-reduce.17
  6132.2 101.7 all-reduce.17
  6275.3 101.6 all-reduce.17
  6418.3 101.6 all-reduce.17
  6561.3 101.7 all-reduce.17
  6704.3 101.7 all-reduce.17
  6847.4 101.6 all-reduce.17
  6990.4 101.6 all-reduce.17
  7133.5 101.7 all-reduce.17
  7276.5 101.6 all-reduce.17
  7419.6 101.6 all-reduce.17
  7562.6 101.7 all-reduce.17
  7705.7 101.7 all-reduce.17
  7848.8 101.7 all-reduce.17
  7991.8 101.7 all-reduce.17
  8134.9 101.6 all-reduce.17
  8277.9 101.6 all-reduce.17
  12519.0 150.7 all-reduce.13
  (80 shorter events, 6846.5 us)
where the time goes:
time: 12700 us
  waiting for transfers between devices  10300 us (81%)
  blocking collectives  1020 us (8%)
  other arithmetic  434 us (3%)
  starting transfers between devices  386 us (3%)
  matrix products  253 us (2%)
  local copies, waits for them, and re-layouts  222 us (2%)
    psum x39, waiting for transfers between devices, bwd_tick(): lax.psum(contract(grad_hidden, w_one, 1, 1), 'tp')  3370 us
    psum x39, waiting for transfers between devices, fwd_tick(): lax.psum(jnp.dot(gate_act, w_two, preferred_element_type=jnp.float32), 'tp')  3240 us
    psum x32, waiting for transfers between devices, head_step(): grad_normed = lax.psum(normed_part, 'tp')  3240 us
    while x32, blocking collectives  1000 us
  transfers between devices with their start and end apart: 190, of which 190 were waited for; matrix products, arithmetic and copies ran while one was open for 1% of the time, Pallas kernels for 0%

commit v1 on v0

v1 whole, which is shorter than its diff:
```python
import jax
import jax.numpy as jnp
from jax import lax
from jax.sharding import PartitionSpec as P

NORM_EPS = 1e-6


def contract(lhs, rhs, lhs_dim, rhs_dim):
    return lax.dot_general(lhs, rhs, (((lhs_dim,), (rhs_dim,)), ((), ())), preferred_element_type=jnp.float32)


def gelu_slope(hidden):
    gate, pull = jax.vjp(jax.nn.gelu, hidden)
    return gate, pull(jnp.ones_like(gate))[0]


def solution(mesh):
    pp_size = mesh.shape['pp']
    tp_size = mesh.shape['tp']
    fwd_perm = [(src, src + 1) for src in range(pp_size - 1)]
    bwd_perm = [(src + 1, src) for src in range(pp_size - 1)]

    def device_fn(tokens, labels, emb_table, w_in, w_out):
        num_tokens = tokens.shape[0] * tokens.shape[1]
        vocab_rows, model_dim = emb_table.shape
        w_one, w_two = w_in[0], w_out[0]
        stage = lax.axis_index('pp')
        is_first = stage == 0
        is_last = stage == pp_size - 1
        base = lax.axis_index('tp') * vocab_rows
        unit = num_tokens // (pp_size * tp_size)

        def reorder(ids):
            return ids.reshape(pp_size, tp_size, unit).transpose(1, 0, 2).reshape(num_tokens)

        tok_local = reorder(tokens) - base
        lab_local = reorder(labels) - base
        row_ids = jnp.arange(vocab_rows, dtype=jnp.int32)

        owned = (tok_local >= 0) & (tok_local < vocab_rows)
        looked = jnp.take(emb_table, jnp.clip(tok_local, 0, vocab_rows - 1), axis=0)
        looked = jnp.where(owned[:, None], looked, jnp.zeros_like(looked))
        x_act = lax.psum_scatter(looked, 'tp', scatter_dimension=0, tiled=True)

        w_one_full = lax.all_gather(w_one, 'tp', axis=1, tiled=True)
        w_two_full = lax.all_gather(w_two, 'tp', axis=0, tiled=True)

        x_mine = jnp.zeros_like(x_act)
        for tick in range(pp_size):
            x_mine = jnp.where(stage == tick, x_act, x_mine)
            gate = jax.nn.gelu(jnp.dot(x_act, w_one_full, preferred_element_type=jnp.float32)).astype(jnp.bfloat16)
            branch = jnp.dot(gate, w_two_full, preferred_element_type=jnp.float32)
            y_act = (x_act.astype(jnp.float32) + branch).astype(jnp.bfloat16)
            if tick < pp_size - 1:
                x_act = lax.ppermute(y_act, 'pp', fwd_perm)

        slope = gelu_slope(jnp.dot(x_mine, w_one_full, preferred_element_type=jnp.float32))[1]

        top = lax.psum(jnp.where(is_last, y_act, jnp.zeros_like(y_act)), 'pp')
        top = lax.all_gather(top, 'tp', axis=0, tiled=True)
        x_wide = top.astype(jnp.float32)
        inv_rms = lax.rsqrt(jnp.mean(x_wide * x_wide, axis=-1, keepdims=True) + NORM_EPS)
        normed = x_wide * inv_rms
        normed_b = normed.astype(jnp.bfloat16)
        hit = lab_local[:, None] == row_ids[None, :]
        logits = contract(normed_b, emb_table, 1, 1)
        local_lse = jax.nn.logsumexp(logits, axis=-1)
        local_target = jnp.sum(jnp.where(hit, logits, 0.0), axis=-1)
        stats = lax.all_gather(jnp.stack([local_lse, local_target]), 'tp')
        log_norm = jax.nn.logsumexp(stats[:, 0], axis=0)
        target_logit = jnp.sum(stats[:, 1], axis=0)
        mean_loss = jnp.sum(log_norm - target_logit) / num_tokens
        grad_logits = (jnp.exp(logits - log_norm[:, None]) - hit.astype(jnp.float32)).astype(jnp.bfloat16)

        def my_part(arr):
            return lax.dynamic_index_in_dim(arr.reshape(tp_size, pp_size, unit, arr.shape[-1]), stage, 1, keepdims=False).reshape(tp_size * unit, arr.shape[-1])

        dn_part = contract(my_part(grad_logits), emb_table, 1, 0)
        dn = lax.psum_scatter(dn_part, 'tp', scatter_dimension=0, tiled=True)
        tp_idx = lax.axis_index('tp')
        m_own = lax.dynamic_slice_in_dim(my_part(normed), tp_idx * unit, unit, 0)
        r_own = lax.dynamic_slice_in_dim(my_part(inv_rms), tp_idx * unit, unit, 0)
        g_own = (r_own * (dn - m_own * jnp.mean(m_own * dn, axis=-1, keepdims=True))).astype(jnp.bfloat16)
        g_act = lax.all_gather(g_own, 'pp', axis=0, tiled=True)

        dy_mine = jnp.zeros_like(g_act)
        for tick in range(pp_size - 1, -1, -1):
            dy_mine = jnp.where(stage == tick, g_act, dy_mine)
            grad_hidden = (slope * contract(g_act, w_two_full, 1, 1)).astype(jnp.bfloat16)
            grad_x = (g_act.astype(jnp.float32) + contract(grad_hidden, w_one_full, 1, 1)).astype(jnp.bfloat16)
            if tick > 0:
                g_act = lax.ppermute(grad_x, 'pp', bwd_perm)

        x_all = lax.all_gather(x_mine, 'tp', axis=0, tiled=True)
        dy_all = lax.all_gather(dy_mine, 'tp', axis=0, tiled=True)
        gate_all, slope_all = gelu_slope(jnp.dot(x_all, w_one, preferred_element_type=jnp.float32))
        dh_all = (slope_all * contract(dy_all, w_two, 1, 1)).astype(jnp.bfloat16)
        grad_two = contract(gate_all.astype(jnp.bfloat16), dy_all, 0, 0)
        grad_one = contract(x_all, dh_all, 0, 0)

        dx_first = lax.psum(jnp.where(is_first, grad_x, jnp.zeros_like(grad_x)), 'pp')
        dx_first = lax.all_gather(dx_first, 'tp', axis=0, tiled=True)
        one_hot = (tok_local[:, None] == row_ids[None, :]).astype(jnp.bfloat16)
        grad_table = contract(grad_logits, normed_b, 0, 0) + contract(one_hot, dx_first, 0, 0)
        return mean_loss.reshape(1), grad_one[None], grad_two[None], grad_table

    return jax.shard_map(device_fn, mesh=mesh, in_specs=(P('dp', None), P('dp', None), P('tp', None), P('pp', None, 'tp'), P('pp', 'tp', None)), out_specs=(P('dp'), P(('dp', 'pp'), None, 'tp'), P(('dp', 'pp'), 'tp', None), P(('dp', 'tp'), None)), check_vma=False)
```

time: 12700 us -> 1110 us (0.09)
  waiting for transfers between devices: 10300 us -> 671 us
  blocking collectives: 1020 us -> 34 us
  other arithmetic: 434 us -> 34.5 us
  starting transfers between devices: 386 us -> 45.8 us
  local copies, waits for them, and re-layouts: 222 us -> 35 us
    psum x112 -> x2, waiting for transfers between devices: 10100 us -> 112 us  [the longest x1 58.4 us: device_fn(): top = lax.psum(jnp.where(is_last, y_act, jnp.zeros_like(y_act)), 'pp')]
    while x32 -> x0, blocking collectives: 1000 us -> none
    all_gather x0 -> x6, waiting for transfers between devices: none -> 349 us  [the longest x1 78.3 us: device_fn(): w_one_full = lax.all_gather(w_one, 'tp', axis=1, tiled=True)]
    ppermute x78 -> x14, starting transfers between devices: 386 us -> 45.4 us  [the longest x7 31.1 us: device_fn(): x_act = lax.ppermute(y_act, 'pp', fwd_perm)]
    dynamic_update_slice x110 -> x0, other arithmetic: 183 us -> none  [the longest x78 126 us: device_fn(): lax.scan(fwd_tick, act_zero, jnp.arange(num_ticks))[1]]
    reduce_scatter x0 -> x2, waiting for transfers between devices: none -> 146 us  [the longest x1 78.5 us: device_fn(): x_act = lax.psum_scatter(looked, 'tp', scatter_dimension=0, tiled=True)]
  transfers between devices with their start and end apart: 190 -> 24, of which waited for: 190 -> 24; matrix products, arithmetic and copies ran while one was open for 1% -> 2% of each run, Pallas kernels for 0% -> 0%
where the time goes in v1:
time: 1110 us
  waiting for transfers between devices  671 us (60%)
  matrix products  268 us (24%)
  starting transfers between devices  45.8 us (4%)
  local copies, waits for them, and re-layouts  35 us (3%)
  other arithmetic  34.5 us (3%)
  blocking collectives  34 us (3%)
  between operations  16.9 us (2%)
    dot_general x14, matrix products, contract(): lax.dot_general(lhs, rhs, (((lhs_dim,), (rhs_dim,)), ((), ())), preferred...  189 us
    reduce_scatter x1, waiting for transfers between devices, device_fn(): x_act = lax.psum_scatter(looked, 'tp', scatter_dimension=0, tiled=True)  78.5 us
    all_gather x1, waiting for transfers between devices, device_fn(): w_one_full = lax.all_gather(w_one, 'tp', axis=1, tiled=True)  78.3 us
    all_gather x1, waiting for transfers between devices, device_fn(): w_two_full = lax.all_gather(w_two, 'tp', axis=0, tiled=True)  73.3 us
    dot_general x8, matrix products, device_fn(): branch = jnp.dot(gate, w_two_full, preferred_element_type=jnp.float32)  68.7 us
    reduce_scatter x1, waiting for transfers between devices, device_fn(): dn = lax.psum_scatter(dn_part, 'tp', scatter_dimension=0, tiled=True)  67.2 us
    psum x1, waiting for transfers between devices, device_fn(): top = lax.psum(jnp.where(is_last, y_act, jnp.zeros_like(y_act)), 'pp')  58.4 us
    all_gather x1, waiting for transfers between devices, device_fn(): x_all = lax.all_gather(x_mine, 'tp', axis=0, tiled=True)  54.9 us
  transfers between devices with their start and end apart: 24, of which 24 were waited for; matrix products, arithmetic and copies ran while one was open for 2% of the time, Pallas kernels for 0%

profile of v1, /device:TPU:1, one launch (start us, length us, event | category | flops | bytes accessed | tf_op | source)
XLA Modules:
  0.0 1105.3 jit_solution(7520355979445573267)
XLA Ops:
  9.0 14.6 %gather_fusion = bf16[2048,1024]{1,0:T(8,128)(2,1)} fusion(bf16[3144,1024]{1,0:T(8,128)(2,1)} %param.7, s32[2048]{0:T(1024)S(1)} %broadcast_clamp_fusion.1), kind=kCustom, calls=%fused_computation | custom fusion | bytes 8396800 | tf_op jit(solution)/shard_map/jit(_take)/gather | solution.py:42
  29.1 78.5 %reduce-scatter.3.cloned.1.call-done = bf16[128,1024]{1,0:T(8,128)(2,1)} async-done(((bf16[2048,1024]{1,0:T(8,128)(2,1)}), bf16[128,1024]{1,0:T(8,128)(2,1)}) %reduce-scatter.3.cloned.1.call-update) | async-done | bytes 262160 | tf_op jit(solution)/shard_map/reduce_scatter | solution.py:44
  107.6 78.3 %all-gather.19.cloned.1.call-done = bf16[1,1024,4096]{2,1,0:T(8,128)(2,1)} async-done(((bf16[1,1024,256]{2,1,0:T(8,128)(2,1)}), bf16[1,1024,4096]{2,1,0:T(8,128)(2,1)}) %all-gather.19.cloned.1.call-update) | async-done | bytes 8388624 | tf_op jit(solution)/shard_map/all_gather | solution.py:46
  186.0 73.3 %all-gather.21.cloned.1.call-done = bf16[1,4096,1024]{2,1,0:T(8,128)(2,1)} async-done(((bf16[1,256,1024]{2,1,0:T(8,128)(2,1)}), bf16[1,4096,1024]{2,1,0:T(8,128)(2,1)}) %all-gather.21.cloned.1.call-update) | async-done | bytes 8388624 | tf_op jit(solution)/shard_map/all_gather | solution.py:47
  259.2 8.6 fusion.237
  275.0 8.5 add_convert_fusion.13
  291.2 8.5 add_convert_fusion.12
  323.6 8.5 add_convert_fusion.10
  372.1 9.2 fusion.283
  381.4 58.4 %all-reduce.3.cloned.1.call-done = bf16[128,1024]{1,0:T(8,128)(2,1)} async-done(((bf16[128,1024]{1,0:T(8,128)(2,1)}), bf16[128,1024]{1,0:T(8,128)(2,1)}) %all-reduce.3.cloned.1.call-update) | async-done | bytes 262160 | tf_op jit(solution)/shard_map/psum | solution.py:60
  440.0 54.0 %all-gather.11.cloned.1.call-done = bf16[2048,1024]{1,0:T(8,128)(2,1)} async-done(((bf16[128,1024]{1,0:T(8,128)(2,1)}), bf16[2048,1024]{1,0:T(8,128)(2,1)}) %all-gather.11.cloned.1.call-update) | async-done | bytes 4194320 | tf_op jit(solution)/shard_map/all_gather | solution.py:61
  497.4 19.6 %fusion.359 = (f32[2048]{0:T(1024)S(1)}, f32[2048,3144]{0,1:T(8,128)}) fusion(bf16[3144,1024]{1,0:T(8,128)(2,1)} %param.7, f32[2048]{0:T(1024)S(1)} %add_rsqrt_fusion, bf16[2048,1024]{1,0:T(8,128)(2,1)S(1)} %copy-done.1), kind=kOutput, calls=%fused_computation.295 | convolution fusion | flops 13199620096 | bytes 36405248 | tf_op jit(solution)/shard_map/dot_general | solution.py:10
  517.0 12.4 %exponential_reduce_fusion = (f32[2048]{0:T(1024)S(1)}, f32[2048]{0:T(1024)S(1)}) fusion(f32[2048,3144]{0,1:T(8,128)} %get-tuple-element.18, f32[2048]{0:T(1024)S(1)} %is-finite_select_fusion.2, s32[2048]{0:T(1024)S(1)} %sub.99), kind=kLoop, calls=%fused_computation.6 | loop fusion | flops 32190464 | bytes 25788416 | tf_op jit(solution)/shard_map/reduce_sum | solution.py:68
  529.4 18.6 %all-gather.3 = f32[16,2,2048]{2,1,0:T(2,128)S(1)} all-gather(f32[1,2,2048]{2,1,0:T(2,128)S(1)} %maximum_bitcast_fusion), channel_id=4, replica_groups=mesh['dp'=1,'tp'=16,'pp'=8] {'tp'}, dimensions={0}, use_global_device_ids=true | all-gather | bytes 278528 | tf_op jit(solution)/shard_map/all_gather | solution.py:70
  557.5 17.2 %copy.16 = bf16[2048,3144]{1,0:T(8,128)(2,1)} copy(bf16[2048,3144]{0,1:T(8,128)(2,1)} %subtract_convert_fusion) | data formatting | bytes 25755648 | tf_op jit(solution)/shard_map/convert_element_type | solution.py:74
  591.6 67.2 %reduce-scatter.5.cloned.1.call-done = f32[16,1024]{1,0:T(8,128)} async-done(((f32[256,1024]{1,0:T(8,128)}), f32[16,1024]{1,0:T(8,128)}) %reduce-scatter.5.cloned.1.call-update) | async-done | bytes 65552 | tf_op jit(solution)/shard_map/reduce_scatter | solution.py:80
  660.7 15.3 %all_gather.33 = bf16[128,1024]{1,0:T(8,128)(2,1)S(1)} all-gather(bf16[16,1024]{1,0:T(8,128)(2,1)S(1)} %multiply_convert_fusion.2), channel_id=1, replica_groups=mesh['dp'=1,'tp'=16,'pp'=8] {'pp'}, dimensions={0}, use_global_device_ids=true | all-gather | bytes 294912 | tf_op jit(solution)/shard_map/all_gather | solution.py:85
  676.0 11.4 %fusion.240 = bf16[128,1024]{1,0:T(8,128)(2,1)S(1)} fusion(bf16[1,1024,4096]{2,1,0:T(8,128)(2,1)} %all-gather.19.cloned.1.call-done, f32[128,4096]{1,0:T(8,128)S(1)} %fusion.129, bf16[128,1024]{1,0:T(8,128)(2,1)S(1)} %all_gather.33, bf16[1,4096,1024]{2,1,0:T(8,128)(2,1)} %all-gather.21.cloned.1.call-done), kind=kOutput, calls=%fused_computation.194 | convolution fusion | flops 2148925440 | bytes 19398656 | tf_op jit(solution)/shard_map/dot_general | solution.py:10
  695.1 11.4 %add_convert_fusion.6 = bf16[128,1024]{1,0:T(8,128)(2,1)S(1)} fusion(bf16[128,1024]{1,0:T(8,128)(2,1)S(1)} %collective-permute-done.7, bf16[1,1024,4096]{2,1,0:T(8,128)(2,1)} %all-gather.19.cloned.1.call-done, f32[128,4096]{1,0:T(8,128)S(1)} %fusion.129, bf16[1,4096,1024]{2,1,0:T(8,128)(2,1)} %all-gather.21.cloned.1.call-done), kind=kOutput, calls=%fused_computation.208 | convolution fusion | flops 2148925440 | bytes 19398656 | tf_op jit(solution)/shard_map/dot_general | solution.py:10
  714.2 11.4 %add_convert_fusion.5 = bf16[128,1024]{1,0:T(8,128)(2,1)S(1)} fusion(bf16[128,1024]{1,0:T(8,128)(2,1)S(1)} %collective-permute-done.8, bf16[1,1024,4096]{2,1,0:T(8,128)(2,1)} %all-gather.19.cloned.1.call-done, f32[128,4096]{1,0:T(8,128)S(1)} %fusion.129, bf16[1,4096,1024]{2,1,0:T(8,128)(2,1)} %all-gather.21.cloned.1.call-done), kind=kOutput, calls=%fused_computation.207 | convolution fusion | flops 2148925440 | bytes 19398656 | tf_op jit(solution)/shard_map/dot_general | solution.py:10
  733.3 12.1 %add_convert_fusion.4 = bf16[128,1024]{1,0:T(8,128)(2,1)} fusion(bf16[128,1024]{1,0:T(8,128)(2,1)S(1)} %collective-permute-done.9, bf16[1,1024,4096]{2,1,0:T(8,128)(2,1)} %all-gather.19.cloned.1.call-done, f32[128,4096]{1,0:T(8,128)S(1)} %fusion.129, bf16[1,4096,1024]{2,1,0:T(8,128)(2,1)} %all-gather.21.cloned.1.call-done), kind=kOutput, calls=%fused_computation.206 | convolution fusion | flops 2148925440 | bytes 19398656 | tf_op jit(solution)/shard_map/dot_general | solution.py:10
  753.1 12.1 %add_convert_fusion.3 = bf16[128,1024]{1,0:T(8,128)(2,1)} fusion(bf16[128,1024]{1,0:T(8,128)(2,1)S(1)} %collective-permute-done.10, bf16[1,1024,4096]{2,1,0:T(8,128)(2,1)} %all-gather.19.cloned.1.call-done, f32[128,4096]{1,0:T(8,128)S(1)} %fusion.129, bf16[1,4096,1024]{2,1,0:T(8,128)(2,1)} %all-gather.21.cloned.1.call-done), kind=kOutput, calls=%fused_computation.205 | convolution fusion | flops 2148925440 | bytes 19398656 | tf_op jit(solution)/shard_map/dot_general | solution.py:10
  773.0 12.2 %add_convert_fusion.2 = bf16[128,1024]{1,0:T(8,128)(2,1)} fusion(bf16[128,1024]{1,0:T(8,128)(2,1)} %collective-permute-done.11, bf16[1,1024,4096]{2,1,0:T(8,128)(2,1)} %all-gather.19.cloned.1.call-done, f32[128,4096]{1,0:T(8,128)S(1)} %fusion.129, bf16[1,4096,1024]{2,1,0:T(8,128)(2,1)} %all-gather.21.cloned.1.call-done), kind=kOutput, calls=%fused_computation.204 | convolution fusion | flops 2148925440 | bytes 19398656 | tf_op jit(solution)/shard_map/dot_general | solution.py:10
  792.9 12.2 %add_convert_fusion.1 = bf16[128,1024]{1,0:T(8,128)(2,1)} fusion(bf16[128,1024]{1,0:T(8,128)(2,1)} %collective-permute-done.12, bf16[1,1024,4096]{2,1,0:T(8,128)(2,1)} %all-gather.19.cloned.1.call-done, f32[128,4096]{1,0:T(8,128)S(1)} %fusion.129, bf16[1,4096,1024]{2,1,0:T(8,128)(2,1)} %all-gather.21.cloned.1.call-done), kind=kOutput, calls=%fused_computation.203 | convolution fusion | flops 2148925440 | bytes 19398656 | tf_op jit(solution)/shard_map/dot_general | solution.py:10
  812.7 12.7 %fusion.284 = (bf16[128,1024]{1,0:T(8,128)(2,1)}, bf16[128,1024]{1,0:T(8,128)(2,1)}) fusion(bf16[128,1024]{1,0:T(8,128)(2,1)} %collective-permute-done.13, pred[]{:T(512)S(6)} %eq.70, bf16[128,1024]{1,0:T(8,128)(2,1)} %collective-permute-done.12, bf16[128,1024]{1,0:T(8,128)(2,1)} %collective-permute-done.11, ...), kind=kOutput, calls=%fused_computation.217 | convolution fusion | flops 2150105088 | bytes 21495816 | tf_op jit(solution)/shard_map/dot_general | solution.py:10
  827.0 54.1 %all-reduce.5.cloned.1.call-done = bf16[128,1024]{1,0:T(8,128)(2,1)} async-done(((bf16[128,1024]{1,0:T(8,128)(2,1)}), bf16[128,1024]{1,0:T(8,128)(2,1)}) %all-reduce.5.cloned.1.call-update) | async-done | bytes 262160 | tf_op jit(solution)/shard_map/psum | solution.py:102
  881.0 54.9 %all-gather.13.cloned.1.call-done = bf16[2048,1024]{1,0:T(8,128)(2,1)} async-done(((bf16[128,1024]{1,0:T(8,128)(2,1)}), bf16[2048,1024]{1,0:T(8,128)(2,1)}) %all-gather.13.cloned.1.call-update) | async-done | bytes 4194320 | tf_op jit(solution)/shard_map/all_gather | solution.py:95
  940.2 49.3 %all-gather.15.cloned.1.call-done = bf16[2048,1024]{1,0:T(8,128)(2,1)} async-done(((bf16[128,1024]{1,0:T(8,128)(2,1)}), bf16[2048,1024]{1,0:T(8,128)(2,1)}) %all-gather.15.cloned.1.call-update) | async-done | bytes 4194320 | tf_op jit(solution)/shard_map/all_gather | solution.py:96
  994.0 9.3 convolution_bitcast_fusion.1
  1003.3 39.0 %all-gather.17.cloned.1.call-done = bf16[2048,1024]{1,0:T(8,128)(2,1)} async-done(((bf16[128,1024]{1,0:T(8,128)(2,1)}), bf16[2048,1024]{1,0:T(8,128)(2,1)}) %all-gather.17.cloned.1.call-update) | async-done | bytes 4194320 | tf_op jit(solution)/shard_map/all_gather | solution.py:103
  1042.3 32.5 %fusion = f32[3144,1024]{1,0:T(8,128)} fusion(bf16[2048,1024]{1,0:T(8,128)(2,1)} %all-gather.17.cloned.1.call-done, s32[2048]{0:T(1024)S(1)} %copy-done.7), kind=kOutput, calls=%fused_computation.2 | convolution fusion | flops 13193330688 | bytes 17080320 | tf_op jit(solution)/shard_map/dot_general | solution.py:10
  1074.8 22.0 %convolution_add_fusion = f32[3144,1024]{1,0:T(8,128)} fusion(f32[3144,1024]{1,0:T(8,128)} %fusion, bf16[2048,3144]{0,1:T(8,128)(2,1)} %subtract_convert_fusion, bf16[2048,1024]{1,0:T(8,128)(2,1)S(1)} %copy-done.2, f32[2048]{0:T(1024)S(1)} %add_rsqrt_fusion), kind=kOutput, calls=%fused_computation.10 | convolution fusion | flops 13196402688 | bytes 42835968 | tf_op jit(solution)/shard_map/dot_general | solution.py:10
  (107 shorter events, 181.2 us)
Async XLA Ops:
  7.2 100.4 %reduce-scatter.3.cloned.1.call-start = ((), (), s32[]{:S(2)}) async-start(), calls=%async_computation.2 | async-start | bytes 4456448 | tf_op jit(solution)/shard_map/reduce_scatter | solution.py:44
  8.2 0.6 copy-start.6
  27.6 158.4 %all-gather.19.cloned.1.call-start = ((), (), s32[]{:S(2)}) async-start(), calls=%async_computation.10 | async-start | bytes 8912896 | tf_op jit(solution)/shard_map/all_gather | solution.py:46
  28.3 230.9 %all-gather.21.cloned.1.call-start = ((), (), s32[]{:S(2)}) async-start(), calls=%async_computation.11 | async-start | bytes 8912896 | tf_op jit(solution)/shard_map/all_gather | solution.py:47
  29.0 410.7 %all-reduce.3.cloned.1.call-start = ((), (), s32[]{:S(2)}) async-start(), calls=%async_computation.3 | async-start | bytes 524288 | tf_op jit(solution)/shard_map/psum | solution.py:60
  267.8 7.2 collective-permute-start
  283.5 7.7 collective-permute-start.1
  299.7 7.7 collective-permute-start.2
  315.9 7.7 collective-permute-start.3
  332.1 7.7 collective-permute-start.4
  348.2 7.7 collective-permute-start.5
  364.4 7.7 collective-permute-start.6
  381.4 112.6 %all-gather.11.cloned.1.call-start = ((), (), s32[]{:S(2)}) async-start(), calls=%async_computation.4 | async-start | bytes 4456448 | tf_op jit(solution)/shard_map/all_gather | solution.py:61
  439.8 219.0 %reduce-scatter.5.cloned.1.call-start = ((), (), s32[]{:S(2)}) async-start(), calls=%async_computation.6 | async-start | bytes 1114112 | tf_op jit(solution)/shard_map/reduce_scatter | solution.py:80
  494.0 3.4 copy-start.1
  517.0 32.1 %copy-start = (f32[2048,3144]{0,1:T(8,128)S(1)}, f32[2048,3144]{0,1:T(8,128)}, u32[]{:S(2)}) copy-start(f32[2048,3144]{0,1:T(8,128)} %get-tuple-element.18) | copy-start | bytes 77266944
  576.2 6.0 copy-start.5
  582.1 298.9 %all-reduce.5.cloned.1.call-start = ((), (), s32[]{:S(2)}) async-start(), calls=%async_computation.8 | async-start | bytes 524288 | tf_op jit(solution)/shard_map/psum | solution.py:102
  582.3 6.1 copy-start.3
  687.4 7.7 collective-permute-start.7
  706.5 7.7 collective-permute-start.8
  725.6 7.7 collective-permute-start.9
  745.5 7.7 collective-permute-start.10
  765.3 7.7 collective-permute-start.11
  785.2 7.7 collective-permute-start.12
  805.1 7.7 collective-permute-start.13
  825.4 110.5 %all-gather.13.cloned.1.call-start = ((), (), s32[]{:S(2)}) async-start(), calls=%async_computation.5 | async-start | bytes 4456448 | tf_op jit(solution)/shard_map/all_gather | solution.py:95
  826.2 163.3 %all-gather.15.cloned.1.call-start = ((), (), s32[]{:S(2)}) async-start(), calls=%async_computation.7 | async-start | bytes 4456448 | tf_op jit(solution)/shard_map/all_gather | solution.py:96
  826.9 215.4 %all-gather.17.cloned.1.call-start = ((), (), s32[]{:S(2)}) async-start(), calls=%async_computation.9 | async-start | bytes 4456448 | tf_op jit(solution)/shard_map/all_gather | solution.py:103
  940.2 53.9 %copy-start.4 = (bf16[1,256,1024]{2,1,0:T(8,128)(2,1)S(1)}, bf16[1,256,1024]{2,1,0:T(8,128)(2,1)}, u32[]{:S(2)}) copy-start(bf16[1,256,1024]{2,1,0:T(8,128)(2,1)} %param.9) | copy-start | bytes 1572868
  994.0 48.3 %copy-start.7 = (s32[2048]{0:T(1024)S(1)}, s32[2048]{0:T(1024)}, u32[]{:S(2)}) copy-start(s32[2048]{0:T(1024)} %copy-done.6) | copy-start | bytes 24580
  1042.3 32.5 %copy-start.2 = (bf16[2048,1024]{1,0:T(8,128)(2,1)S(1)}, bf16[2048,1024]{1,0:T(8,128)(2,1)}, u32[]{:S(2)}) copy-start(bf16[2048,1024]{1,0:T(8,128)(2,1)} %all-gather.11.cloned.1.call-done) | copy-start | bytes 12582916
Sparse Core Ops, SparseCore 0:
  27.7 79.8 reduce-scatter.2
  109.7 76.1 all-gather.18
  188.1 71.0 all-gather.20
  381.5 58.2 all-reduce.2
  441.8 52.1 all-gather.10
  582.2 76.5 reduce-scatter.4
  825.6 55.4 all-reduce.4
  883.7 52.1 all-gather.12
  938.7 50.7 all-gather.14
  991.5 50.7 all-gather.16

commit v2 on v1

v2 whole, which is shorter than its diff:
```python
import functools

import jax
import jax.numpy as jnp
from jax import lax
from jax.experimental import pallas as pl
from jax.experimental.pallas import tpu as pltpu
from jax.sharding import PartitionSpec as P

NORM_EPS = 1e-6
SIDE = 4
MESH = pl.DeviceIdType.MESH
F32 = jnp.float32
BF16 = jnp.bfloat16
VMEM_LIMIT = 63 * 1024 * 1024
CUBE = 0.044715
ROOT = 0.7978845608028654


def contract(lhs, rhs, lhs_dim, rhs_dim):
    return lax.dot_general(lhs, rhs, (((lhs_dim,), (rhs_dim,)), ((), ())), preferred_element_type=F32)


def gelu(h):
    return h * (0.5 * (1.0 + jnp.tanh(ROOT * (h + CUBE * (h * h * h)))))


def gelu_slope(h):
    sq = h * h
    t = jnp.tanh(ROOT * (h + CUBE * (sq * h)))
    return 0.5 * (1.0 + t) + (0.5 * h) * (1.0 - t * t) * (ROOT * (1.0 + (3.0 * CUBE) * sq))


def remote(src, dst, send, recv, where):
    return pltpu.make_async_remote_copy(src_ref=src, dst_ref=dst, send_sem=send, recv_sem=recv, device_id=where, device_id_type=MESH)


def signal(peer):
    pl.semaphore_signal(pltpu.get_barrier_semaphore(), inc=1, device_id=peer, device_id_type=MESH)


class Plane:
    def __init__(self):
        self.tp = lax.axis_index('tp')
        self.y = lax.rem(self.tp, SIDE)
        self.z = self.tp // SIDE

    def at(self, dy, dz):
        return lax.rem(self.z + dz + SIDE, SIDE) * SIDE + lax.rem(self.y + dy + SIDE, SIDE)

    def blk(self, half, df, ds):
        return self.at(df, ds) if half == 0 else self.at(ds, df)

    def near(self):
        return [{'tp': self.at(1, 0)}, {'tp': self.at(-1, 0)}, {'tp': self.at(0, 1)}, {'tp': self.at(0, -1)}]

    def rings(self):
        return [{'tp': self.at(d, 0)} for d in (1, 2, 3)] + [{'tp': self.at(0, d)} for d in (1, 2, 3)]


HOPS = (0, -1, 1, 2)
SLOTS = 20


def plane_gather(plane, bufs, send_sem, recv_sem, lo, on_block):
    def msg(a, half, slot, df, ds, part, to):
        buf, base, count = bufs[a]
        size = count // 2
        start = base + half * size
        if part is not None:
            size = size // 2
            start = start + part * size
        ref = buf.at[plane.blk(half, df, ds), pl.ds(start, size)]
        k = (a * 2 + half) * SLOTS + slot
        return remote(ref, ref, send_sem.at[k], recv_sem.at[k], {'tp': plane.blk(half, *to)})

    def f(a, half, slot, sending):
        if slot == 0:
            return msg(a, half, 0, 0 if sending else -1, 0, None, (1, 0))
        if slot == 1:
            return msg(a, half, 1, 0 if sending else 1, 0, None, (-1, 0))
        if slot == 2:
            return msg(a, half, 2, -1 if sending else 2, 0, 0, (1, 0))
        return msg(a, half, 3, 1 if sending else 2, 0, 1, (-1, 0))

    def s(a, half, j, k, sending):
        df = HOPS[j]
        slot = 4 + 4 * j + k
        if k == 0:
            return msg(a, half, slot, df, 0 if sending else -1, None, (0, 1))
        if k == 1:
            return msg(a, half, slot, df, 0 if sending else 1, None, (0, -1))
        if k == 2:
            return msg(a, half, slot, df, -1 if sending else 2, 0, (0, 1))
        return msg(a, half, slot, df, 1 if sending else 2, 1, (0, -1))

    pairs = [(a, half) for a in range(len(bufs)) for half in (0, 1)]
    for a, half in pairs:
        for slot in (0, 1):
            f(a, half, slot, True).start()
        for k in (0, 1):
            s(a, half, 0, k, True).start()
        on_block(a, half, 0, 0)
    for a, half in pairs:
        for slot, j in ((0, 1), (1, 2)):
            f(a, half, slot, False).wait_recv()
            f(a, half, slot + 2, True).start()
            for k in (0, 1):
                s(a, half, j, k, True).start()
            on_block(a, half, j, 0)
    for a, half in pairs:
        for k in (0, 1):
            s(a, half, 0, k, False).wait_recv()
            s(a, half, 0, k + 2, True).start()
            on_block(a, half, 0, k + 1)
    for a, half in pairs:
        f(a, half, 2, False).wait_recv()
        f(a, half, 3, False).wait_recv()
        for k in (0, 1):
            s(a, half, 3, k, True).start()
        on_block(a, half, 3, 0)
    for j in (1, 2, 3):
        for a, half in pairs:
            for k in (0, 1):
                s(a, half, j, k, False).wait_recv()
                s(a, half, j, k + 2, True).start()
                on_block(a, half, j, k + 1)
    for j in range(4):
        for a, half in pairs:
            s(a, half, j, 2, False).wait_recv()
            s(a, half, j, 3, False).wait_recv()
            on_block(a, half, j, 3)

    def finish():
        for a, half in pairs:
            for slot in range(4):
                f(a, half, slot, True).wait_send()
            for j in range(4):
                for k in range(4):
                    s(a, half, j, k, True).wait_send()

    return finish


def local(src, dst, sem):
    return pltpu.make_async_copy(src, dst, sem)


def forward_kernel(last, x_first, w_one, w_two, x_out, y_out, slope_ref, one_out, two_out, ones, twos, x_buf, y_buf, a_buf, send_sem, recv_sem, hop_sem, loc_sem):
    plane = Plane()
    stage = lax.axis_index('pp')
    tp = plane.tp
    own_one = local(w_one, ones.at[tp], loc_sem.at[0])
    own_two = local(w_two, twos.at[tp], loc_sem.at[1])
    own_one.start()
    own_two.start()
    after = {'pp': lax.rem(stage + 1, last + 1)}
    before = {'pp': lax.rem(stage + last, last + 1)}
    peers = plane.near() + [after, before]
    for peer in peers:
        signal(peer)
    own_one.wait()
    own_two.wait()
    pl.semaphore_wait(pltpu.get_barrier_semaphore(), len(peers))
    finish = plane_gather(plane, [(ones, 0, ones.shape[1]), (twos, 0, twos.shape[1])], send_sem, recv_sem, 0, lambda *_: None)
    save_one = local(ones, one_out, loc_sem.at[0])
    save_two = local(twos, two_out, loc_sem.at[1])
    save_one.start()
    save_two.start()
    hop = remote(y_buf, x_buf, hop_sem.at[0], hop_sem.at[1], after)

    @pl.when(stage == 0)
    def _():
        x_buf[...] = x_first[...]

    @pl.when(stage > 0)
    def _():
        hop.wait_recv()

    x_act = x_buf[...]
    blocks, _, cols = ones.shape
    for k in range(blocks):
        hidden = jnp.dot(x_act, ones[k], preferred_element_type=F32)
        slope_ref[k] = hidden
        a_buf[:, k * cols:(k + 1) * cols] = gelu(hidden).astype(BF16)
    gate = a_buf[...]
    wide = x_act.shape[1]
    for n in range(0, wide, 256):
        branch = jnp.dot(gate, twos[:, :, n:n + 256].reshape(blocks * cols, 256), preferred_element_type=F32)
        y_buf[:, n:n + 256] = (x_buf[:, n:n + 256].astype(F32) + branch).astype(BF16)

    @pl.when(stage < last)
    def _():
        hop.start()

    y_out[...] = y_buf[...]
    x_out[...] = x_buf[...]
    for k in range(blocks):
        slope_ref[k] = gelu_slope(slope_ref[k])
    finish()
    save_one.wait()
    save_two.wait()

    @pl.when(stage < last)
    def _():
        hop.wait_send()


def backward_kernel(last, g_top, slope_ref, one_all, two_all, dy_out, dx_out, ones, twos, dy_buf, dx_buf, d_buf, hop_sem, one_sem, two_sem):
    stage = lax.axis_index('pp')
    blocks, _, cols = one_all.shape
    loads_two = [local(two_all.at[k], twos.at[k], two_sem.at[k]) for k in range(blocks)]
    loads_one = [local(one_all.at[k], ones.at[:, pl.ds(k * cols, cols)], one_sem.at[k]) for k in range(blocks)]
    for load in loads_two + loads_one:
        load.start()
    after = {'pp': lax.rem(stage + 1, last + 1)}
    before = {'pp': lax.rem(stage + last, last + 1)}
    signal(after)
    signal(before)
    pl.semaphore_wait(pltpu.get_barrier_semaphore(), 2)
    hop = remote(dx_buf, dy_buf, hop_sem.at[0], hop_sem.at[1], before)
    for load in loads_two:
        load.wait()

    @pl.when(stage == last)
    def _():
        dy_buf[...] = g_top[...]

    @pl.when(stage < last)
    def _():
        hop.wait_recv()

    grad_y = dy_buf[...]
    for k in range(blocks):
        grad_gate = contract(grad_y, twos[k], 1, 1)
        d_buf[:, k * cols:(k + 1) * cols] = (slope_ref[k] * grad_gate).astype(BF16)
    for load in loads_one:
        load.wait()
    grad_hidden = d_buf[...]
    for n in range(0, grad_y.shape[1], 256):
        back = contract(grad_hidden, ones[n:n + 256, :], 1, 1)
        dx_buf[:, n:n + 256] = (dy_buf[:, n:n + 256].astype(F32) + back).astype(BF16)

    @pl.when(stage > 0)
    def _():
        hop.start()

    dy_out[...] = dy_buf[...]
    dx_out[...] = dx_buf[...]

    @pl.when(stage > 0)
    def _():
        hop.wait_send()


def spread_kernel(source, stages, y_ref, out, line_send, line_recv, send_sem, recv_sem, die_send, die_recv):
    plane = Plane()
    stage = lax.axis_index('pp')
    core = lax.rem(stage, 2)
    mate = {'pp': stage + 1 - 2 * core}
    tp = plane.tp
    rows = y_ref.shape[0] // 2
    lo = pl.multiple_of(core * rows, rows)
    others = [p for p in range(stages) if p != source]
    near = plane.near()
    for peer in near:
        signal(peer)
    twin = source ^ 1

    @pl.when(stage == source)
    def _():
        for p in others:
            signal({'pp': p})

    @pl.when(stage != source)
    def _():
        signal({'pp': source})

    @pl.when((stage != source) & (stage != twin))
    def _():
        signal(mate)

    extra = jnp.where(stage == source, len(others), jnp.where(stage == twin, 1, 2))
    pl.semaphore_wait(pltpu.get_barrier_semaphore(), len(near) + extra)

    def line(p):
        part = pl.ds((p % 2) * rows, rows)
        return remote(y_ref.at[part], out.at[tp, part], line_send.at[p], line_recv, {'pp': p})

    @pl.when(stage == source)
    def _():
        for p in others:
            line(p).start()
        out[tp, pl.ds(lo, rows)] = y_ref[pl.ds(lo, rows)]

    @pl.when(stage != source)
    def _():
        mine = out.at[tp, pl.ds(lo, rows)]
        remote(mine, mine, line_recv, line_recv, mate).wait_recv()

    half_rows = rows // 2

    def die(half, j, k, other):
        df = HOPS[j]
        ds = (0, -1, 1, 2)[k]
        start = (pl.multiple_of((1 - core) * rows, rows) if other else lo) + half * half_rows
        ref = out.at[plane.blk(half, df, ds), pl.ds(start, half_rows)]
        n = half * 16 + j * 4 + k
        return remote(ref, ref, die_send.at[n], die_recv.at[n], mate)

    finish = plane_gather(plane, [(out, lo, rows)], send_sem, recv_sem, lo, lambda a, half, j, k: die(half, j, k, False).start())
    for half in (0, 1):
        for j in range(4):
            for k in range(4):
                die(half, j, k, True).wait_recv()
    for half in (0, 1):
        for j in range(4):
            for k in range(4):
                die(half, j, k, False).wait_send()
    finish()

    @pl.when(stage == source)
    def _():
        for p in others:
            line(p).wait_send()


def share_kernel(stats, out, send_sem, recv_sem):
    tp = lax.axis_index('tp')
    size = out.shape[0]
    for d in range(1, size):
        signal({'tp': lax.rem(tp + d, size)})
    out[tp] = stats[...]
    pl.semaphore_wait(pltpu.get_barrier_semaphore(), size - 1)

    def msg(d, block):
        return remote(stats, out.at[block], send_sem.at[d], recv_sem.at[d], {'tp': lax.rem(tp + d, size)})

    for d in range(1, size):
        msg(d, tp).start()
    for d in range(1, size):
        msg(d, lax.rem(tp + size - d, size)).wait_recv()
    for d in range(1, size):
        msg(d, tp).wait_send()


def reduce_kernel(target, stages, head, parts, own_x, out, got_one, sum_one, got_two, piece, one_send, one_recv, two_send, two_recv, line_send, line_recv):
    plane = Plane()
    stage = lax.axis_index('pp')
    ring = plane.rings()
    others = [p for p in range(stages) if p != target]
    for peer in ring:
        signal(peer)

    @pl.when(stage == target)
    def _():
        for p in others:
            signal({'pp': p})
        pl.semaphore_wait(pltpu.get_barrier_semaphore(), len(ring) + len(others))

    @pl.when(stage != target)
    def _():
        signal({'pp': target})
        pl.semaphore_wait(pltpu.get_barrier_semaphore(), len(ring) + 1)

    width = parts.shape[3]
    half_cols = width // 2
    y, z = plane.y, plane.z

    def cols(half):
        return pl.ds(half * half_cols, half_cols)

    def row(half, index):
        return parts.at[:, index, :, cols(half)] if half == 0 else parts.at[index, :, :, cols(half)]

    def first(half, d):
        dest = lax.rem((y if half == 0 else z) + d, SIDE)
        n = half * 3 + d - 1
        return remote(row(half, dest), got_one.at[n], one_send.at[n], one_recv.at[n], {'tp': plane.blk(half, d, 0)})

    def second(half, d):
        dest = lax.rem((z if half == 0 else y) + d, SIDE)
        n = half * 3 + d - 1
        return remote(sum_one.at[half, dest], got_two.at[n], two_send.at[n], two_recv.at[n], {'tp': plane.blk(half, 0, d)})

    for d in (2, 1, 3):
        for half in (0, 1):
            first(half, d).start()
    for half in (0, 1):
        total = row(half, y if half == 0 else z)[...].astype(F32)
        for d in (1, 3, 2):
            first(half, d).wait_recv()
            total = total + got_one[half * 3 + d - 1].astype(F32)
        sum_one[half] = total.astype(sum_one.dtype)
        for d in (2, 1, 3):
            second(half, d).start()
    sums = []
    for half in (0, 1):
        total = sum_one[half, z if half == 0 else y].astype(F32)
        for d in (1, 3, 2):
            second(half, d).wait_recv()
            total = total + got_two[half * 3 + d - 1].astype(F32)
        sums.append(total)
    if head:
        x_wide = own_x[...].astype(F32)
        inv_rms = lax.rsqrt(jnp.mean(x_wide * x_wide, axis=-1, keepdims=True) + NORM_EPS)
        normed = x_wide * inv_rms
        mean = (jnp.sum(normed[:, :half_cols] * sums[0], axis=-1, keepdims=True) + jnp.sum(normed[:, half_cols:] * sums[1], axis=-1, keepdims=True)) / width
        sums = [inv_rms * (sums[h] - normed[:, h * half_cols:(h + 1) * half_cols] * mean) for h in (0, 1)]
    for half in (0, 1):
        piece[:, half * half_cols:(half + 1) * half_cols] = sums[half].astype(BF16)

    def line(p):
        return remote(piece, out.at[p], line_send, line_recv.at[p], {'pp': target})

    @pl.when(stage != target)
    def _():
        line(stage).start()

    @pl.when(stage == target)
    def _():
        out[target] = piece[...]
        for p in others:
            line(p).wait_recv()

    for half in (0, 1):
        for d in (1, 2, 3):
            first(half, d).wait_send()
            second(half, d).wait_send()

    @pl.when(stage != target)
    def _():
        line(stage).wait_send()


def collect_kernel(x_ref, dy_ref, x_all, dy_all, send_sem, recv_sem):
    plane = Plane()
    near = plane.near()
    for peer in near:
        signal(peer)
    x_all[plane.tp] = x_ref[...]
    dy_all[plane.tp] = dy_ref[...]
    pl.semaphore_wait(pltpu.get_barrier_semaphore(), len(near))
    plane_gather(plane, [(x_all, 0, x_all.shape[1]), (dy_all, 0, dy_all.shape[1])], send_sem, recv_sem, 0, lambda *_: None)()


def vmem():
    return pl.BlockSpec(memory_space=pltpu.VMEM)


def anywhere():
    return pl.BlockSpec(memory_space=pl.ANY)


def params(cid):
    return pltpu.CompilerParams(collective_id=cid, has_side_effects=True, vmem_limit_bytes=VMEM_LIMIT)


DMA = pltpu.SemaphoreType.DMA


def solution(mesh):
    pp_size = mesh.shape['pp']
    tp_size = mesh.shape['tp']
    last = pp_size - 1

    def device_fn(tokens, labels, emb_table, w_in, w_out):
        num_tokens = tokens.shape[0] * tokens.shape[1]
        vocab_rows, width = emb_table.shape
        w_one, w_two = w_in[0], w_out[0]
        cols = w_one.shape[1]
        stage = lax.axis_index('pp')
        tp_idx = lax.axis_index('tp')
        base = tp_idx * vocab_rows
        unit = num_tokens // (pp_size * tp_size)
        block = pp_size * unit
        shape = jax.ShapeDtypeStruct

        def reorder(ids):
            return ids.reshape(pp_size, tp_size, unit).transpose(1, 0, 2).reshape(num_tokens)

        def my_part(arr):
            return lax.dynamic_index_in_dim(arr.reshape(tp_size, pp_size, unit, arr.shape[-1]), stage, 1, keepdims=False)

        tok_local = reorder(tokens) - base
        lab_local = reorder(labels) - base
        row_ids = jnp.arange(vocab_rows, dtype=jnp.int32)

        def reduce_call(parts, own_x, target, head, cid):
            dtype = parts.dtype
            half = width // 2
            return pl.pallas_call(
                functools.partial(reduce_kernel, target, pp_size, head),
                out_shape=shape((pp_size, unit, width), BF16),
                in_specs=[vmem(), vmem()], out_specs=vmem(),
                scratch_shapes=[pltpu.VMEM((6, SIDE, unit, half), dtype), pltpu.VMEM((2, SIDE, unit, half), dtype), pltpu.VMEM((6, unit, half), dtype),
                                pltpu.VMEM((unit, width), BF16), DMA((6,)), DMA((6,)), DMA((6,)), DMA((6,)), DMA, DMA((pp_size,))],
                compiler_params=params(cid), name='reduce_head' if head else 'reduce_lookup',
            )(parts.reshape(SIDE, SIDE, unit, width), own_x).reshape(block, width)

        def spread_call(arr, source, cid):
            return pl.pallas_call(
                functools.partial(spread_kernel, source, pp_size),
                out_shape=shape((tp_size, block, width), BF16),
                in_specs=[vmem()], out_specs=vmem(),
                scratch_shapes=[DMA((pp_size,)), DMA, DMA((2 * SLOTS,)), DMA((2 * SLOTS,)), DMA((32,)), DMA((32,))],
                compiler_params=params(cid), name=f'spread_{source}',
            )(arr).reshape(num_tokens, width)

        tok_part = my_part(tok_local[:, None]).reshape(tp_size * unit)
        owned = (tok_part >= 0) & (tok_part < vocab_rows)
        looked = jnp.take(emb_table, jnp.clip(tok_part, 0, vocab_rows - 1), axis=0)
        looked = jnp.where(owned[:, None], looked, jnp.zeros_like(looked))
        x_first = reduce_call(looked, looked[:unit], 0, False, 1)

        x_mine, y_act, slope, ones, twos = pl.pallas_call(
            functools.partial(forward_kernel, last),
            out_shape=(shape((block, width), BF16), shape((block, width), BF16), shape((tp_size, block, cols), F32),
                       shape((tp_size, width, cols), BF16), shape((tp_size, cols, width), BF16)),
            in_specs=[vmem(), anywhere(), anywhere()],
            out_specs=(vmem(), vmem(), vmem(), anywhere(), anywhere()),
            scratch_shapes=[pltpu.VMEM((tp_size, width, cols), BF16), pltpu.VMEM((tp_size, cols, width), BF16), pltpu.VMEM((block, width), BF16),
                            pltpu.VMEM((block, width), BF16), pltpu.VMEM((block, tp_size * cols), BF16),
                            DMA((4 * SLOTS,)), DMA((4 * SLOTS,)), DMA((2,)), DMA((2,))],
            compiler_params=params(2), name='forward_chain',
        )(x_first, w_one, w_two)

        top = spread_call(y_act, last, 3)
        x_wide = top.astype(F32)
        inv_rms = lax.rsqrt(jnp.mean(x_wide * x_wide, axis=-1, keepdims=True) + NORM_EPS)
        normed_b = (x_wide * inv_rms).astype(BF16)
        hit = lab_local[:, None] == row_ids[None, :]
        logits = contract(normed_b, emb_table, 1, 1)
        local_lse = jax.nn.logsumexp(logits, axis=-1)
        local_target = jnp.sum(jnp.where(hit, logits, 0.0), axis=-1)
        stats = jnp.concatenate([local_lse.reshape(-1, 128), local_target.reshape(-1, 128)], axis=0)
        shared = pl.pallas_call(
            share_kernel, out_shape=shape((tp_size,) + stats.shape, F32), in_specs=[vmem()], out_specs=vmem(),
            scratch_shapes=[DMA((tp_size,)), DMA((tp_size,))], compiler_params=params(4), name='share_stats',
        )(stats).reshape(tp_size, 2, num_tokens)
        log_norm = jax.nn.logsumexp(shared[:, 0], axis=0)
        target_logit = jnp.sum(shared[:, 1], axis=0)
        mean_loss = jnp.sum(log_norm - target_logit) / num_tokens
        grad_logits = (jnp.exp(logits - log_norm[:, None]) - hit.astype(F32)).astype(BF16)
        dn_part = contract(my_part(grad_logits).reshape(tp_size * unit, vocab_rows), emb_table, 1, 0)
        own_x = lax.dynamic_slice_in_dim(top, tp_idx * block + stage * unit, unit, 0)
        g_act = reduce_call(dn_part, own_x, last, True, 5)

        dy_mine, grad_x = pl.pallas_call(
            functools.partial(backward_kernel, last),
            out_shape=(shape((block, width), BF16), shape((block, width), BF16)),
            in_specs=[vmem(), vmem(), anywhere(), anywhere()], out_specs=(vmem(), vmem()),
            scratch_shapes=[pltpu.VMEM((width, tp_size * cols), BF16), pltpu.VMEM((tp_size, cols, width), BF16), pltpu.VMEM((block, width), BF16),
                            pltpu.VMEM((block, width), BF16), pltpu.VMEM((block, tp_size * cols), BF16), DMA((2,)), DMA((tp_size,)), DMA((tp_size,))],
            compiler_params=params(6), name='backward_chain',
        )(g_act, slope, ones, twos)

        x_all, dy_all = pl.pallas_call(
            collect_kernel, out_shape=(shape((tp_size, block, width), BF16),) * 2, in_specs=[vmem(), vmem()], out_specs=(vmem(), vmem()),
            scratch_shapes=[DMA((4 * SLOTS,)), DMA((4 * SLOTS,))], compiler_params=params(7), name='collect',
        )(x_mine, dy_mine)
        x_all, dy_all = x_all.reshape(num_tokens, width), dy_all.reshape(num_tokens, width)
        hidden_all = jnp.dot(x_all, w_one, preferred_element_type=F32)
        dh_all = (gelu_slope(hidden_all) * contract(dy_all, w_two, 1, 1)).astype(BF16)
        grad_two = contract(gelu(hidden_all).astype(BF16), dy_all, 0, 0)
        grad_one = contract(x_all, dh_all, 0, 0)

        dx_first = spread_call(grad_x, 0, 8)
        one_hot = (tok_local[:, None] == row_ids[None, :]).astype(BF16)
        grad_table = contract(grad_logits, normed_b, 0, 0) + contract(one_hot, dx_first, 0, 0)
        return mean_loss.reshape(1), grad_one[None], grad_two[None], grad_table

    return jax.shard_map(device_fn, mesh=mesh, in_specs=(P('dp', None), P('dp', None), P('tp', None), P('pp', None, 'tp'), P('pp', 'tp', None)), out_specs=(P('dp'), P(('dp', 'pp'), None, 'tp'), P(('dp', 'pp'), 'tp', None), P(('dp', 'tp'), None)), check_vma=False)
```

time: 1110 us -> 526 us (0.47)
  the two profiles are of different devices: /device:TPU:1 before, /device:TPU:4 now
where the time goes in v2:
time: 526 us; the launch traced here: 519 us
  Pallas kernels  370 us (70%)
  matrix products  85 us (16%)
  other arithmetic  34.7 us (7%)
  local copies, waits for them, and re-layouts  26.1 us (5%)
    pallas_call x1, Pallas kernels, device_fn(): pl.pallas_call(functools.partial(forward_kernel, last), out_shape=(shape(...  121 us
    pallas_call x2, Pallas kernels, spread_call(): pl.pallas_call(functools.partial(spread_kernel, source, pp_size), out_sha...  107 us
    dot_general x6, matrix products, contract(): lax.dot_general(lhs, rhs, (((lhs_dim,), (rhs_dim,)), ((), ())), preferred...  80.2 us
    pallas_call x1, Pallas kernels, device_fn(): pl.pallas_call(collect_kernel, out_shape=(shape((tp_size, block, width),...  52.8 us
    pallas_call x1, Pallas kernels, device_fn(): pl.pallas_call(functools.partial(backward_kernel, last), out_shape=(shape...  43.8 us
    pallas_call x2, Pallas kernels, reduce_call(): pl.pallas_call(functools.partial(reduce_kernel, target, pp_size, head), o...  34.8 us
    convert_element_type x1, local copies, waits for them, and re-layouts, device_fn(): (jnp.exp(logits - log_norm[:, None]) - hit.astype(F32)).astype(BF16)  16.8 us
    convert_element_type x1, other arithmetic, device_fn(): (jnp.exp(logits - log_norm[:, None]) - hit.astype(F32)).astype(BF16)  15.6 us

profile of v2, /device:TPU:4, one launch (start us, length us, event | category | flops | bytes accessed | tf_op | source)
XLA Modules:
  0.0 519.2 jit_solution(9731845527532120075)
XLA Ops:
  0.6 0.7 broadcast_subtract_fusion
  1.5 0.1 sub.81
  1.7 0.1 and.31
  2.1 5.2 %gather_fusion = bf16[256,1024]{1,0:T(8,128)(2,1)S(1)} fusion(bf16[3144,1024]{1,0:T(8,128)(2,1)} %param.7, s32[1024]{0:T(1024)S(1)} %pad_clamp_fusion), kind=kCustom, calls=%fused_computation | custom fusion | bytes 1049600 | tf_op jit(solution)/shard_map/jit(_take)/gather | solution.py:512
  7.3 0.7 fusion.21.own_x
  8.0 0.9 select_select_fusion.parts
  8.9 17.2 %reduce_lookup.1 = bf16[8,16,1024]{2,1,0:T(8,128)(2,1)} custom-call(bf16[4,4,16,1024]{3,2,1,0:T(8,128)(2,1)} %select_select_fusion.parts, bf16[16,1024]{1,0:T(8,128)(2,1)} %fusion.21.own_x), custom_call_target="tpu_custom_call" | custom-call | tf_op jit(solution)/shard_map/reduce_lookup/pallas_call | solution.py:492
  26.2 120.6 %forward_chain.1 = (bf16[128,1024]{1,0:T(8,128)(2,1)}, bf16[128,1024]{1,0:T(8,128)(2,1)}, f32[16,128,256]{2,1,0:T(8,128)}, bf16[16,1024,256]{2,1,0:T(8,128)(2,1)}, bf16[16,256,1024]{2,1,0:T(8,128)(2,1)}) custom-call(bf16[128,1024]{1,0:T(8,128)(2,1)} %bitcast.69, bf16[1024,256]{1,0:T(8,128)(2,1)} %bitcast.70, bf16[256,1024]{1,0:T(8,128)(2,1)} %bitcast.71), custom_call_target="tpu_custom_call" | custom-call | tf_op jit(solution)/shard_map/forward_chain/pallas_call | solution.py:516
  146.7 44.6 %spread_7.1 = bf16[16,128,1024]{2,1,0:T(8,128)(2,1)} custom-call(bf16[128,1024]{1,0:T(8,128)(2,1)} %get-tuple-element.13.y_ref), custom_call_target="tpu_custom_call" | custom-call | tf_op jit(solution)/shard_map/spread_7/pallas_call | solution.py:502
  191.4 3.2 multiply_reduce_fusion
  194.6 0.2 copy-done
  194.8 0.6 constant_dynamic-slice_fusion.own_x
  195.4 19.5 %fusion.36 = (f32[2048]{0:T(1024)S(1)}, f32[2048,3144]{0,1:T(8,128)}) fusion(bf16[3144,1024]{1,0:T(8,128)(2,1)} %param.7, bf16[2048,1024]{1,0:T(8,128)(2,1)S(1)} %bitcast.62, f32[2048]{0:T(1024)S(1)} %rsqrt_bitcast_fusion), kind=kOutput, calls=%fused_computation.77 | convolution fusion | flops 13199620096 | bytes 36405248 | tf_op jit(solution)/shard_map/dot_general | solution.py:21
  214.9 11.9 %exponential_reduce_fusion = (f32[2048]{0:T(1024)S(1)}, f32[2048]{0:T(1024)S(1)}) fusion(f32[2048,3144]{0,1:T(8,128)} %get-tuple-element.30, f32[2048]{0:T(1024)S(1)} %is-finite_select_fusion.2, s32[2048]{0:T(1024)S(1)} %sub.81), kind=kLoop, calls=%fused_computation.6 | loop fusion | flops 32190464 | bytes 25788416 | tf_op jit(solution)/shard_map/reduce_sum | solution.py:534
  226.8 0.6 pad_maximum_fusion.stats
  227.4 10.9 %share_stats.1 = f32[16,32,128]{2,1,0:T(8,128)} custom-call(f32[32,128]{1,0:T(8,128)} %pad_maximum_fusion.stats), custom_call_target="tpu_custom_call" | custom-call | tf_op jit(solution)/shard_map/share_stats/pallas_call | solution.py:537
  238.4 1.1 reshape.214
  239.4 0.3 slice_reduce_fusion
  239.8 0.6 subtract_reduce_fusion
  241.1 15.6 %subtract_convert_fusion = bf16[2048,3144]{0,1:T(8,128)(2,1)} fusion(f32[2048,3144]{0,1:T(8,128)} %get-tuple-element.30, f32[2048]{0:T(1024)S(1)} %get-tuple-element.27, s32[2048]{0:T(1024)S(1)} %sub.81), kind=kLoop, calls=%fused_computation.3 | loop fusion | flops 32194560 | bytes 38649856 | tf_op jit(solution)/shard_map/convert_element_type | solution.py:544
  256.7 16.8 %copy.11 = bf16[2048,3144]{1,0:T(8,128)(2,1)} copy(bf16[2048,3144]{0,1:T(8,128)(2,1)} %subtract_convert_fusion) | data formatting | bytes 25755648 | tf_op jit(solution)/shard_map/convert_element_type | solution.py:544
  273.5 1.5 constant_dynamic-slice_fusion.1
  275.0 5.9 %fusion.2.parts = f32[4,4,16,1024]{3,2,1,0:T(8,128)} fusion(bf16[3144,1024]{1,0:T(8,128)(2,1)} %param.7, bf16[4,4,16,3144]{3,2,1,0:T(8,128)(2,1)S(1)} %bitcast.67), kind=kOutput, calls=%fused_computation.11 | convolution fusion | flops 1648361472 | bytes 9097216 | tf_op jit(solution)/shard_map/dot_general | solution.py:21
  280.9 17.5 %reduce_head.1 = bf16[8,16,1024]{2,1,0:T(8,128)(2,1)} custom-call(f32[4,4,16,1024]{3,2,1,0:T(8,128)} %fusion.2.parts, bf16[16,1024]{1,0:T(8,128)(2,1)} %constant_dynamic-slice_fusion.own_x), custom_call_target="tpu_custom_call" | custom-call | tf_op jit(solution)/shard_map/reduce_head/pallas_call | solution.py:492
  298.5 43.8 %backward_chain.1 = (bf16[128,1024]{1,0:T(8,128)(2,1)}, bf16[128,1024]{1,0:T(8,128)(2,1)}) custom-call(bf16[128,1024]{1,0:T(8,128)(2,1)} %bitcast.68, f32[16,128,256]{2,1,0:T(8,128)} %get-tuple-element.15.slope_ref, bf16[16,1024,256]{2,1,0:T(8,128)(2,1)} %get-tuple-element.16.one_all, bf16[16,256,1024]{2,1,0:T(8,128)(2,1)} %get-tuple-element.17.two_all), custom_call_target="tpu_custom_call" | custom-call | tf_op jit(solution)/shard_map/backward_chain/pallas_call | solution.py:549
  342.3 62.8 %spread_0.1 = bf16[16,128,1024]{2,1,0:T(8,128)(2,1)} custom-call(bf16[128,1024]{1,0:T(8,128)(2,1)} %get-tuple-element.21.y_ref), custom_call_target="tpu_custom_call" | custom-call | tf_op jit(solution)/shard_map/spread_0/pallas_call | solution.py:502
  405.1 52.8 %collect.1 = (bf16[16,128,1024]{2,1,0:T(8,128)(2,1)}, bf16[16,128,1024]{2,1,0:T(8,128)(2,1)}) custom-call(bf16[128,1024]{1,0:T(8,128)(2,1)} %get-tuple-element.14.x_ref, bf16[128,1024]{1,0:T(8,128)(2,1)} %get-tuple-element.18.dy_ref), custom_call_target="tpu_custom_call" | custom-call | tf_op jit(solution)/shard_map/collect/pallas_call | solution.py:558
  458.0 4.8 fusion.25
  462.8 9.9 %convolution_bitcast_fusion.1 = f32[1,1024,256]{2,1,0:T(8,128)} fusion(bf16[2048,1024]{1,0:T(8,128)(2,1)} %bitcast.83, bf16[2048,1024]{1,0:T(8,128)(2,1)} %bitcast.80, f32[2048,256]{1,0:T(8,128)} %fusion.25, bf16[1,256,1024]{2,1,0:T(8,128)(2,1)S(1)} %copy-done.4), kind=kOutput, calls=%fused_computation.30 | convolution fusion | flops 2156920832 | bytes 12058624 | tf_op jit(solution)/shard_map/dot_general | solution.py:21
  472.7 4.7 convolution_bitcast_fusion
  477.4 18.1 %fusion = f32[3144,1024]{1,0:T(8,128)} fusion(bf16[2048,1024]{1,0:T(8,128)(2,1)S(1)} %bitcast.65, s32[2048]{0:T(1024)S(1)} %sub.90), kind=kOutput, calls=%fused_computation.2 | convolution fusion | flops 13193330688 | bytes 17080320 | tf_op jit(solution)/shard_map/dot_general | solution.py:21
  495.5 22.1 %convolution_add_fusion = f32[3144,1024]{1,0:T(8,128)} fusion(f32[3144,1024]{1,0:T(8,128)} %fusion, bf16[2048,3144]{0,1:T(8,128)(2,1)} %subtract_convert_fusion, bf16[2048,1024]{1,0:T(8,128)(2,1)S(1)} %bitcast.63, f32[2048]{0:T(1024)S(1)} %rsqrt_bitcast_fusion), kind=kOutput, calls=%fused_computation.8 | convolution fusion | flops 13196402688 | bytes 42835968 | tf_op jit(solution)/shard_map/dot_general | solution.py:21
  (29 shorter events, 0.6 us)
Async XLA Ops:
  191.3 3.5 copy-start
  342.3 115.7 %copy-start.3 = (bf16[1,1024,256]{2,1,0:T(8,128)(2,1)S(1)}, bf16[1,1024,256]{2,1,0:T(8,128)(2,1)}, u32[]{:S(2)}) copy-start(bf16[1,1024,256]{2,1,0:T(8,128)(2,1)} %param.8) | copy-start | bytes 1572868
  457.9 4.8 copy-start.4
  462.8 9.9 %copy-start.5 = (f32[2048,256]{1,0:T(8,128)S(1)}, f32[2048,256]{1,0:T(8,128)}, u32[]{:S(2)}) copy-start(f32[2048,256]{1,0:T(8,128)} %fusion.25) | copy-start | bytes 6291460
  472.7 4.7 copy-start.2
  477.4 18.1 %copy-start.1 = (bf16[16,128,1024]{2,1,0:T(8,128)(2,1)S(1)}, bf16[16,128,1024]{2,1,0:T(8,128)(2,1)}, u32[]{:S(2)}) copy-start(bf16[16,128,1024]{2,1,0:T(8,128)(2,1)} %spread_7.1) | copy-start | bytes 12582916

commit v3 on v1

v3 whole, which is shorter than its diff:
```python
import functools

import jax
import jax.numpy as jnp
from jax import lax
from jax.experimental import pallas as pl
from jax.experimental.pallas import tpu as pltpu
from jax.sharding import PartitionSpec as P

NORM_EPS = 1e-6
SIDE = 4
MESH = pl.DeviceIdType.MESH
F32 = jnp.float32
BF16 = jnp.bfloat16
VMEM_LIMIT = 63 * 1024 * 1024
CUBE = 0.044715
ROOT = 0.7978845608028654


def contract(lhs, rhs, lhs_dim, rhs_dim):
    return lax.dot_general(lhs, rhs, (((lhs_dim,), (rhs_dim,)), ((), ())), preferred_element_type=F32)


def gelu(h):
    return h * (0.5 * (1.0 + jnp.tanh(ROOT * (h + CUBE * (h * h * h)))))


def gelu_slope(h):
    sq = h * h
    t = jnp.tanh(ROOT * (h + CUBE * (sq * h)))
    return 0.5 * (1.0 + t) + (0.5 * h) * (1.0 - t * t) * (ROOT * (1.0 + (3.0 * CUBE) * sq))


def remote(src, dst, send, recv, where):
    return pltpu.make_async_remote_copy(src_ref=src, dst_ref=dst, send_sem=send, recv_sem=recv, device_id=where, device_id_type=MESH)


def signal(peer):
    pl.semaphore_signal(pltpu.get_barrier_semaphore(), inc=1, device_id=peer, device_id_type=MESH)


class Plane:
    def __init__(self):
        self.tp = lax.axis_index('tp')
        self.y = lax.rem(self.tp, SIDE)
        self.z = self.tp // SIDE

    def at(self, dy, dz):
        return lax.rem(self.z + dz + SIDE, SIDE) * SIDE + lax.rem(self.y + dy + SIDE, SIDE)

    def blk(self, half, df, ds):
        return self.at(df, ds) if half == 0 else self.at(ds, df)

    def near(self):
        return [{'tp': self.at(1, 0)}, {'tp': self.at(-1, 0)}, {'tp': self.at(0, 1)}, {'tp': self.at(0, -1)}]

    def rings(self):
        return [{'tp': self.at(d, 0)} for d in (1, 2, 3)] + [{'tp': self.at(0, d)} for d in (1, 2, 3)]


HOPS = (0, -1, 1, 2)
WALK = ((0, -1, None, 1), (0, 1, None, -1), (-1, 2, 0, 1), (1, 2, 1, -1))
BOTH = (0, 1)
SLOTS = 20


def plane_gather(plane, bufs, send_sem, recv_sem, on_block=lambda *_: None):
    def msg(a, half, slot, block, part, to):
        buf, start, size = bufs[a]
        size = size // 2
        start = start + half * size
        if part is not None:
            size = size // 2
            start = start + part * size
        ref = buf.at[plane.blk(half, *block), pl.ds(start, size)]
        k = (a * 2 + half) * SLOTS + slot
        return remote(ref, ref, send_sem.at[k], recv_sem.at[k], {'tp': plane.blk(half, *to)})

    def f(a, half, k, end):
        step = WALK[k]
        return msg(a, half, k, (step[end], 0), step[2], (step[3], 0))

    def s(a, half, j, k, end):
        step = WALK[k]
        return msg(a, half, SIDE * (j + 1) + k, (HOPS[j], step[end]), step[2], (0, step[3]))

    send, recv = BOTH
    pairs = [(a, half) for a in range(len(bufs)) for half in BOTH]

    def across(a, half, j):
        for k in BOTH:
            s(a, half, j, k, send).start()
        on_block(a, half, j, 0)

    def onward(a, half, j):
        for k in BOTH:
            s(a, half, j, k, recv).wait_recv()
            s(a, half, j, k + 2, send).start()
            on_block(a, half, j, k + 1)

    for pair in pairs:
        for k in BOTH:
            f(*pair, k, send).start()
        across(*pair, 0)
    yield
    for pair in pairs:
        for k in BOTH:
            f(*pair, k, recv).wait_recv()
            f(*pair, k + 2, send).start()
            across(*pair, k + 1)
    yield
    for pair in pairs:
        onward(*pair, 0)
    yield
    for pair in pairs:
        for k in BOTH:
            f(*pair, k + 2, recv).wait_recv()
        across(*pair, SIDE - 1)
    yield
    for j in range(1, SIDE):
        for pair in pairs:
            onward(*pair, j)
        yield
    for j in range(SIDE):
        for pair in pairs:
            for k in BOTH:
                s(*pair, j, k + 2, recv).wait_recv()
            on_block(*pair, j, SIDE - 1)
    for pair in pairs:
        for k in range(SIDE):
            f(*pair, k, send).wait_send()
            for j in range(SIDE):
                s(*pair, j, k, send).wait_send()


def drain(steps):
    for _ in steps:
        pass


def local(src, dst, sem):
    return pltpu.make_async_copy(src, dst, sem)


class Reduce:
    def __init__(self, plane, parts, got_one, sum_one, got_two, one_send, one_recv, two_send, two_recv):
        self.plane, self.parts, self.got_one, self.sum_one, self.got_two = plane, parts, got_one, sum_one, got_two
        self.one_send, self.one_recv, self.two_send, self.two_recv = one_send, one_recv, two_send, two_recv

    def row(self, half, index):
        size = self.parts.shape[3] // 2
        cols = pl.ds(half * size, size)
        return self.parts.at[:, index, :, cols] if half == 0 else self.parts.at[index, :, :, cols]

    def here(self, half):
        return (self.plane.y, self.plane.z) if half == 0 else (self.plane.z, self.plane.y)

    def first(self, half, d):
        n = half * 3 + d - 1
        dest = lax.rem(self.here(half)[0] + d, SIDE)
        return remote(self.row(half, dest), self.got_one.at[n], self.one_send.at[n], self.one_recv.at[n], {'tp': self.plane.blk(half, d, 0)})

    def second(self, half, d):
        n = half * 3 + d - 1
        dest = lax.rem(self.here(half)[1] + d, SIDE)
        return remote(self.sum_one.at[half, dest], self.got_two.at[n], self.two_send.at[n], self.two_recv.at[n], {'tp': self.plane.blk(half, 0, d)})

    def begin(self):
        for d in (2, 1, 3):
            for half in BOTH:
                self.first(half, d).start()

    def middle(self):
        for half in BOTH:
            total = self.row(half, self.here(half)[0])[:].astype(F32)
            for d in (1, 3, 2):
                self.first(half, d).wait_recv()
                total = total + self.got_one[half * 3 + d - 1].astype(F32)
            self.sum_one[half] = total.astype(self.sum_one.dtype)
            for d in (2, 1, 3):
                self.second(half, d).start()

    def end(self):
        sums = []
        for half in BOTH:
            total = self.sum_one[half, self.here(half)[1]].astype(F32)
            for d in (1, 3, 2):
                self.second(half, d).wait_recv()
                total = total + self.got_two[half * 3 + d - 1].astype(F32)
            sums.append(total)
        return sums

    def close(self):
        for half in BOTH:
            for d in (1, 2, 3):
                self.first(half, d).wait_send()
                self.second(half, d).wait_send()


def greet(peers):
    for peer in peers:
        signal(peer)
    pl.semaphore_wait(pltpu.get_barrier_semaphore(), len(peers))


def forward_kernel(last, swap, ids, emb, w_one, w_two, x_out, y_out, slope_ref, one_out, two_out, ones, twos, one_t, two_t, table, hot, parts,
                   got_one, sum_one, got_two, piece, x_buf, y_buf, a_buf, send_sem, recv_sem, one_send, one_recv, two_send, two_recv, line_send, line_recv, hop_sem, loc_sem):
    plane = Plane()
    stage = lax.axis_index('pp')
    tp = plane.tp
    stages = last + 1
    own_one = local(w_one, ones.at[tp], loc_sem.at[0])
    own_two = local(w_two, twos.at[tp], loc_sem.at[1])
    load = local(emb, table, loc_sem.at[2])
    own_one.start()
    own_two.start()
    load.start()
    for peer in plane.rings() + [{'pp': lax.rem(stage + d, stages)} for d in range(1, stages)]:
        signal(peer)
    own_one.wait()
    own_two.wait()
    pl.semaphore_wait(pltpu.get_barrier_semaphore(), 6 + last)
    gather = plane_gather(plane, [(ones, 0, ones.shape[1]), (twos, 0, twos.shape[1])], send_sem, recv_sem)
    next(gather)

    rows, width = table.shape
    group, full = hot.shape
    load.wait()
    row_ids = ids[:]
    lanes = lax.broadcasted_iota(jnp.int32, (group, full), 1)
    hot[:] = jnp.where(row_ids == lanes, 1.0, 0.0).astype(BF16)
    tail = jnp.where(row_ids == full + lax.broadcasted_iota(jnp.int32, (group, rows - full), 1), 1.0, 0.0).astype(BF16)
    for n in range(0, width, 256):
        picked = jnp.dot(hot[:], table[:full, n:n + 256], preferred_element_type=F32) + jnp.dot(tail, table[full:, n:n + 256], preferred_element_type=F32)
        parts[:, :, :, n:n + 256] = picked.astype(BF16).reshape(parts.shape[:3] + (256,))
    red = Reduce(plane, parts, got_one, sum_one, got_two, one_send, one_recv, two_send, two_recv)
    red.begin()
    next(gather)
    red.middle()
    next(gather)
    unit = piece.shape[0]
    for half, total in enumerate(red.end()):
        piece[:, half * (width // 2):(half + 1) * (width // 2)] = total.astype(BF16)

    def line(p):
        return remote(piece, x_buf.at[pl.ds(pl.multiple_of(p * unit, unit), unit)], line_send, line_recv.at[p], {'pp': 0})

    @pl.when(stage != 0)
    def _():
        line(stage).start()

    @pl.when(stage == 0)
    def _():
        x_buf[:unit] = piece[:]

    drain(gather)

    blocks, _, cols = ones.shape
    save_one = local(one_t, one_out, loc_sem.at[3])
    save_two = local(two_t, two_out, loc_sem.at[4])

    def turn():
        @pl.loop(0, blocks)
        def _(k):
            one_t[k] = ones[k].T
            two_t[k] = twos[k].T

        save_one.start()
        save_two.start()

    pl.when(stage >= swap)(turn)
    hop = remote(y_buf, x_buf, hop_sem.at[0], hop_sem.at[1], {'pp': lax.rem(stage + 1, stages)})

    @pl.when(stage == 0)
    def _():
        for p in range(1, stages):
            line(p).wait_recv()

    @pl.when(stage > 0)
    def _():
        hop.wait_recv()

    x_act = x_buf[:]
    for k in range(blocks):
        hidden = jnp.dot(x_act, ones[k], preferred_element_type=F32)
        slope_ref[k] = hidden
        a_buf[:, k * cols:(k + 1) * cols] = gelu(hidden).astype(BF16)
    gate = a_buf[:]
    for n in range(0, width, 256):
        branch = jnp.dot(gate, twos[:, :, n:n + 256].reshape(blocks * cols, 256), preferred_element_type=F32)
        y_buf[:, n:n + 256] = (x_buf[:, n:n + 256].astype(F32) + branch).astype(BF16)

    @pl.when(stage < last)
    def _():
        hop.start()

    y_out[:] = y_buf[:]
    x_out[:] = x_buf[:]
    for k in range(blocks):
        slope_ref[k] = gelu_slope(slope_ref[k])
    pl.when(stage < swap)(turn)
    red.close()
    save_one.wait()
    save_two.wait()

    @pl.when(stage != 0)
    def _():
        line(stage).wait_send()

    @pl.when(stage < last)
    def _():
        hop.wait_send()


def norm_of(x):
    wide = x.astype(F32)
    inv_rms = lax.rsqrt(jnp.mean(wide * wide, axis=-1, keepdims=True) + NORM_EPS)
    return inv_rms, wide * inv_rms


def spread_kernel(source, stages, head, y_ref, out, *refs):
    if head:
        own_out, n_buf, own_send, own_recv, line_send, line_recv, send_sem, recv_sem, die_send, die_recv = refs
    else:
        line_send, line_recv, send_sem, recv_sem, die_send, die_recv = refs
    plane = Plane()
    stage = lax.axis_index('pp')
    core = lax.rem(stage, 2)
    mate = {'pp': stage + 1 - 2 * core}
    tp = plane.tp
    rows = y_ref.shape[0] // 2
    lo = pl.multiple_of(core * rows, rows)
    others = [p for p in range(stages) if p != source]
    near = plane.near()
    for peer in near:
        signal(peer)
    twin = source ^ 1

    @pl.when(stage == source)
    def _():
        for p in others:
            signal({'pp': p})

    @pl.when(stage != source)
    def _():
        signal({'pp': source})

    @pl.when((stage != source) & (stage != twin))
    def _():
        signal(mate)

    if head:
        n_buf[:] = norm_of(y_ref[:])[1].astype(BF16)
        src = n_buf
        unit = own_out.shape[0]
    else:
        src = y_ref
    extra = jnp.where(stage == source, len(others), jnp.where(stage == twin, 1, 2))
    pl.semaphore_wait(pltpu.get_barrier_semaphore(), len(near) + extra)

    def line(p):
        part = pl.ds((p % 2) * rows, rows)
        return remote(src.at[part], out.at[tp, part], line_send.at[p], line_recv, {'pp': p})

    def own(p):
        return remote(y_ref.at[pl.ds(p * unit, unit)], own_out, own_send.at[p], own_recv, {'pp': p})

    @pl.when(stage == source)
    def _():
        for p in others:
            line(p).start()
        out[tp, pl.ds(lo, rows)] = src[pl.ds(lo, rows)]
        if head:
            for p in others:
                own(p).start()
            own_out[:] = y_ref[source * unit:(source + 1) * unit]

    @pl.when(stage != source)
    def _():
        mine = out.at[tp, pl.ds(lo, rows)]
        remote(mine, mine, line_recv, line_recv, mate).wait_recv()

    half_rows = rows // 2

    def die(half, j, k, other):
        df = HOPS[j]
        ds = HOPS[k]
        start = (pl.multiple_of((1 - core) * rows, rows) if other else lo) + half * half_rows
        ref = out.at[plane.blk(half, df, ds), pl.ds(start, half_rows)]
        n = half * 16 + j * 4 + k
        return remote(ref, ref, die_send.at[n], die_recv.at[n], mate)

    drain(plane_gather(plane, [(out, lo, rows)], send_sem, recv_sem, lambda a, half, j, k: die(half, j, k, False).start()))
    for half in BOTH:
        for j in range(4):
            for k in range(4):
                die(half, j, k, True).wait_recv()
    for half in BOTH:
        for j in range(4):
            for k in range(4):
                die(half, j, k, False).wait_send()

    @pl.when(stage == source)
    def _():
        for p in others:
            line(p).wait_send()
            if head:
                own(p).wait_send()

    if head:
        @pl.when(stage != source)
        def _():
            remote(own_out, own_out, own_recv, own_recv, mate).wait_recv()


def fold(op, value):
    rows, cols = value.shape
    return op(value.reshape(rows // 8, 8, cols), axis=0)


def head_kernel(target, stages, chunk, emb, top, lab, lab_two, own_x, x_mine, loss_out, g_out, n_out, g_top, x_all,
                table, n_buf, e_buf, g_buf, peak, stat, shared, scale_ref, parts, got_one, sum_one, got_two, piece,
                send_sem, recv_sem, share_send, share_recv, one_send, one_recv, two_send, two_recv, line_send, line_recv, loc_sem):
    plane = Plane()
    stage = lax.axis_index('pp')
    tp = plane.tp
    size = shared.shape[0]
    others = [p for p in range(stages) if p != target]
    load = local(emb, table, loc_sem.at[0])
    load.start()
    for d in range(1, size):
        signal({'tp': lax.rem(tp + d, size)})

    @pl.when(stage == target)
    def _():
        for p in others:
            signal({'pp': p})

    @pl.when(stage != target)
    def _():
        signal({'pp': target})

    x_all[tp] = x_mine[:]
    group = peak.shape[1]
    unit = group // size
    for p in range(stages):
        n_buf[p * group:(p + 1) * group] = top[:, p * unit:(p + 1) * unit, :].reshape(group, top.shape[2])
    pl.semaphore_wait(pltpu.get_barrier_semaphore(), size - 1 + jnp.where(stage == target, len(others), 1))
    gather = plane_gather(plane, [(x_all, 0, x_all.shape[1])], send_sem, recv_sem)
    next(gather)
    save_n = local(n_buf, n_out, loc_sem.at[1])
    save_n.start()
    load.wait()

    rows, width = table.shape
    full = rows // chunk
    pieces = e_buf.shape[0]
    pair = e_buf.shape[2]

    def logit_chunk(b, start, count):
        logits = contract(table[pl.ds(start, count), :], n_buf[b * pair:(b + 1) * pair, :], 1, 1)
        e_buf[b, pl.ds(start, count), :] = logits
        return fold(jnp.max, logits)

    def exp_chunk(b, start, count, top_b, total, hits):
        logits = e_buf[b, pl.ds(start, count), :]
        hit = lab_two[b:b + 1, :] == start + lax.broadcasted_iota(jnp.int32, logits.shape, 0)
        e = jnp.exp(logits - top_b)
        e_buf[b, pl.ds(start, count), :] = e
        return total + fold(jnp.sum, e), hits + fold(jnp.sum, jnp.where(hit, logits, 0.0))

    top_b = None
    zero = jnp.zeros((8, pair), F32)
    for b in range(pieces + 1):
        def both(start, count, carry, b=b, top_b=top_b):
            best, total, hits = carry
            if b < pieces:
                best = jnp.maximum(best, logit_chunk(b, start, count))
            if b > 0:
                total, hits = exp_chunk(b - 1, start, count, top_b, total, hits)
            return best, total, hits

        carry = (jnp.full((8, pair), -jnp.inf, F32), zero, zero)
        carry = lax.fori_loop(0, full, lambda c, carry: both(pl.multiple_of(c * chunk, chunk), chunk, carry), carry)
        best, total, hits = both(full * chunk, rows - full * chunk, carry)
        if b > 0:
            lse = top_b + jnp.log(jnp.sum(total, axis=0, keepdims=True))
            hits = jnp.sum(hits, axis=0, keepdims=True)
            for i in range(pair // group):
                p = (b - 1) * (pair // group) + i
                stat[0, p:p + 1, :] = lse[:, i * group:(i + 1) * group]
                stat[1, p:p + 1, :] = hits[:, i * group:(i + 1) * group]
                peak[p:p + 1, :] = top_b[:, i * group:(i + 1) * group]
        if b < pieces:
            top_b = jnp.max(best, axis=0, keepdims=True)
            for _ in range((1, 2, 1, 2)[b]):
                next(gather)

    def msg(d, block):
        return remote(stat, shared.at[block], share_send.at[d], share_recv.at[d], {'tp': lax.rem(tp + d, size)})

    for d in range(1, size):
        msg(d, tp).start()
    shared[tp] = stat[:]
    drain(gather)
    for d in range(1, size):
        msg(d, lax.rem(tp + size - d, size)).wait_recv()
    every = shared[:, 0]
    most = jnp.max(every, axis=0)
    log_norm = most + jnp.log(jnp.sum(jnp.exp(every - most[None]), axis=0))
    loss_out[:] = jnp.sum(log_norm - jnp.sum(shared[:, 1], axis=0), keepdims=True)
    scale_ref[:] = jnp.exp(peak[:] - log_norm)

    def grad_block(p, slot):
        b = p // (pair // group)
        col = pl.multiple_of(lax.rem(p, pair // group) * group, group)
        factor = scale_ref[pl.ds(p, 1), :]
        label = lab[pl.ds(p, 1), :]

        def part(start, count):
            e = e_buf[b, pl.ds(start, count), pl.ds(col, group)]
            hit = label == start + lax.broadcasted_iota(jnp.int32, e.shape, 0)
            g_buf[slot, pl.ds(start, count), :] = (e * factor - jnp.where(hit, 1.0, 0.0)).astype(BF16)

        @pl.loop(0, full)
        def _(c):
            part(pl.multiple_of(c * chunk, chunk), chunk)

        part(full * chunk, rows - full * chunk)

    def save(p, slot):
        return local(g_buf.at[slot], g_out.at[:, pl.ds(pl.multiple_of(p * group, group), group)], loc_sem.at[2 + slot])

    grad_block(stage, 0)
    cut = full * chunk
    for n in range(0, width, 256):
        back = contract(g_buf[0, :cut, :], table[:cut, n:n + 256], 0, 0) + contract(g_buf[0, cut:, :], table[cut:, n:n + 256], 0, 0)
        parts[:, :, :, n:n + 256] = back.reshape(parts.shape[:3] + (256,))
    red = Reduce(plane, parts, got_one, sum_one, got_two, one_send, one_recv, two_send, two_recv)
    red.begin()
    save(stage, 0).start()
    for k in range(1, stages):
        p = lax.rem(stage + k, stages)
        slot = k % 2
        if k >= 2:
            save(p, slot).wait()
        grad_block(p, slot)
        save(p, slot).start()
    red.middle()
    sums = red.end()
    inv_rms, normed = norm_of(own_x[:])
    half = width // 2
    mean = (jnp.sum(normed[:, :half] * sums[0], axis=-1, keepdims=True) + jnp.sum(normed[:, half:] * sums[1], axis=-1, keepdims=True)) / width
    for h in BOTH:
        piece[:, h * half:(h + 1) * half] = (inv_rms * (sums[h] - normed[:, h * half:(h + 1) * half] * mean)).astype(BF16)

    def line(p):
        return remote(piece, g_top.at[p], line_send, line_recv.at[p], {'pp': target})

    @pl.when(stage != target)
    def _():
        line(stage).start()

    @pl.when(stage == target)
    def _():
        g_top[target] = piece[:]
        for p in others:
            line(p).wait_recv()

    red.close()
    for d in range(1, size):
        msg(d, tp).wait_send()
    save_n.wait()
    save(stage, 0).wait()
    save(stage, 1).wait()

    @pl.when(stage != target)
    def _():
        line(stage).wait_send()


def backward_kernel(last, early, chunk, g_top, slope_ref, one_all, two_all, g_all, n_all, dx_out, dy_all, de_out,
                    ones, twos, g_buf, n_buf, de_buf, dy_buf, dx_buf, d_buf, send_sem, recv_sem, hop_sem, loc_sem):
    plane = Plane()
    stage = lax.axis_index('pp')
    blocks, cols, width = one_all.shape
    loads = [local(two_all, twos, loc_sem.at[0]), local(one_all, ones, loc_sem.at[1]), local(g_all, g_buf, loc_sem.at[2]), local(n_all, n_buf, loc_sem.at[3])]
    for load in loads:
        load.start()
    after = {'pp': lax.rem(stage + 1, last + 1)}
    before = {'pp': lax.rem(stage + last, last + 1)}
    greet(plane.near() + [after, before])
    hop = remote(dx_buf, dy_buf, hop_sem.at[0], hop_sem.at[1], before)
    save = local(de_buf, de_out, loc_sem.at[4])
    rows = de_buf.shape[0]
    full = rows // chunk

    def table_part(start, count):
        de_buf[pl.ds(start, count), :] = jnp.dot(g_buf[pl.ds(start, count), :], n_buf[:], preferred_element_type=F32)

    def table_parts(lo, hi):
        @pl.loop(lo, hi)
        def _(c):
            table_part(pl.multiple_of(c * chunk, chunk), chunk)

    @pl.when(stage <= early)
    def _():
        loads[2].wait()
        loads[3].wait()
        table_parts(0, full)
        table_part(full * chunk, rows - full * chunk)
        save.start()

    loads[0].wait()

    @pl.when(stage == last)
    def _():
        dy_buf[:] = g_top[:]

    @pl.when(stage < last)
    def _():
        hop.wait_recv()

    grad_y = dy_buf[:]
    for k in range(blocks):
        grad_gate = jnp.dot(grad_y, twos[k], preferred_element_type=F32)
        d_buf[:, k * cols:(k + 1) * cols] = (slope_ref[k] * grad_gate).astype(BF16)
    loads[1].wait()
    grad_hidden = d_buf[:]
    for n in range(0, width, 256):
        back = jnp.dot(grad_hidden, ones[:, :, n:n + 256].reshape(blocks * cols, 256), preferred_element_type=F32)
        dx_buf[:, n:n + 256] = (dy_buf[:, n:n + 256].astype(F32) + back).astype(BF16)

    @pl.when(stage > 0)
    def _():
        hop.start()

    dx_out[:] = dx_buf[:]
    dy_all[plane.tp] = dy_buf[:]

    def gather():
        return plane_gather(plane, [(dy_all, 0, dy_all.shape[1])], send_sem, recv_sem)

    @pl.when(stage <= early)
    def _():
        drain(gather())

    @pl.when(stage > early)
    def _():
        steps = gather()
        next(steps)
        loads[2].wait()
        loads[3].wait()
        for c in range(full):
            table_parts(c, c + 1)
            next(steps)
        table_part(full * chunk, rows - full * chunk)
        save.start()
        drain(steps)

    save.wait()

    @pl.when(stage > 0)
    def _():
        hop.wait_send()


def weight_kernel(x_ref, dy_ref, one_ref, two_ref, out_one, out_two):
    @pl.when(pl.program_id(0) == 0)
    def _():
        out_one[:] = jnp.zeros_like(out_one)
        out_two[:] = jnp.zeros_like(out_two)

    x_act, grad_y = x_ref[:], dy_ref[:]
    hidden = jnp.dot(x_act, one_ref[:], preferred_element_type=F32)
    grad_gate = contract(grad_y, two_ref[:], 1, 1)
    grad_hidden = (gelu_slope(hidden) * grad_gate).astype(BF16)
    out_one[:] += contract(x_act, grad_hidden, 0, 0)
    out_two[:] += contract(gelu(hidden).astype(BF16), grad_y, 0, 0)


def vmem():
    return pl.BlockSpec(memory_space=pltpu.VMEM)


def anywhere():
    return pl.BlockSpec(memory_space=pl.ANY)


def params(cid):
    return pltpu.CompilerParams(collective_id=cid, has_side_effects=True, vmem_limit_bytes=VMEM_LIMIT)


DMA = pltpu.SemaphoreType.DMA


def solution(mesh):
    pp_size = mesh.shape['pp']
    tp_size = mesh.shape['tp']
    last = pp_size - 1

    def device_fn(tokens, labels, emb_table, w_in, w_out):
        num_tokens = tokens.shape[0] * tokens.shape[1]
        vocab_rows, width = emb_table.shape
        w_one, w_two = w_in[0], w_out[0]
        cols = w_one.shape[1]
        stage = lax.axis_index('pp')
        base = lax.axis_index('tp') * vocab_rows
        unit = num_tokens // (pp_size * tp_size)
        block = pp_size * unit
        group = tp_size * unit
        half = width // 2
        chunk = 512
        pair = 2 * group
        shape = jax.ShapeDtypeStruct
        VM = pltpu.VMEM

        tok_local = tokens.reshape(num_tokens) - base
        lab_local = labels.reshape(num_tokens) - base
        ids = lax.dynamic_slice_in_dim(tok_local, stage * group, group)[:, None]

        def reduce_scratch(dtype):
            return [VM((SIDE, SIDE, unit, width), dtype), VM((6, SIDE, unit, half), dtype), VM((2, SIDE, unit, half), dtype), VM((6, unit, half), dtype), VM((unit, width), BF16)]

        reduce_sems = [DMA((6,)), DMA((6,)), DMA((6,)), DMA((6,)), DMA, DMA((pp_size,))]

        x_mine, y_act, slope, one_t, two_t = pl.pallas_call(
            functools.partial(forward_kernel, last, pp_size // 2),
            out_shape=(shape((block, width), BF16), shape((block, width), BF16), shape((tp_size, block, cols), F32),
                       shape((tp_size, cols, width), BF16), shape((tp_size, width, cols), BF16)),
            in_specs=[vmem(), anywhere(), anywhere(), anywhere()],
            out_specs=(vmem(), vmem(), vmem(), anywhere(), anywhere()),
            scratch_shapes=[VM((tp_size, width, cols), BF16), VM((tp_size, cols, width), BF16), VM((tp_size, cols, width), BF16), VM((tp_size, width, cols), BF16),
                            VM((vocab_rows, width), BF16), VM((group, vocab_rows // chunk * chunk), BF16), *reduce_scratch(BF16),
                            VM((block, width), BF16), VM((block, width), BF16), VM((block, tp_size * cols), BF16),
                            DMA((4 * SLOTS,)), DMA((4 * SLOTS,)), *reduce_sems, DMA((2,)), DMA((5,))],
            compiler_params=params(1), name='forward_chain',
        )(ids, emb_table, w_one, w_two)

        def spread_call(arr, source, head, cid):
            out = shape((tp_size, block, width), BF16)
            sems = [DMA((pp_size,)), DMA, DMA((2 * SLOTS,)), DMA((2 * SLOTS,)), DMA((32,)), DMA((32,))]
            return pl.pallas_call(
                functools.partial(spread_kernel, source, pp_size, head),
                out_shape=(out, shape((unit, width), BF16)) if head else out,
                in_specs=[vmem()], out_specs=(vmem(), vmem()) if head else vmem(),
                scratch_shapes=[VM((block, width), BF16), DMA((pp_size,)), DMA, *sems] if head else sems,
                compiler_params=params(cid), name=f'spread_{source}',
            )(arr)

        top, own_x = spread_call(y_act, last, True, 2)
        loss, g_all, n_all, g_top, x_all = pl.pallas_call(
            functools.partial(head_kernel, last, pp_size, chunk),
            out_shape=(shape((1, 1), F32), shape((vocab_rows, num_tokens), BF16), shape((num_tokens, width), BF16), shape((pp_size, unit, width), BF16), shape((tp_size, block, width), BF16)),
            in_specs=[anywhere(), vmem(), vmem(), vmem(), vmem(), vmem()],
            out_specs=(vmem(), anywhere(), anywhere(), vmem(), vmem()),
            scratch_shapes=[VM((vocab_rows, width), BF16), VM((num_tokens, width), BF16), VM((num_tokens // pair, vocab_rows, pair), F32), VM((2, vocab_rows, group), BF16),
                            VM((pp_size, group), F32), VM((2, pp_size, group), F32), VM((tp_size, 2, pp_size, group), F32), VM((pp_size, group), F32), *reduce_scratch(F32),
                            DMA((2 * SLOTS,)), DMA((2 * SLOTS,)), DMA((tp_size,)), DMA((tp_size,)), *reduce_sems, DMA((4,))],
            compiler_params=params(3), name='head',
        )(emb_table, top, lab_local.reshape(pp_size, group), lab_local.reshape(num_tokens // pair, pair), own_x, x_mine)

        grad_x, dy_all, de_head = pl.pallas_call(
            functools.partial(backward_kernel, last, 4, chunk),
            out_shape=(shape((block, width), BF16), shape((tp_size, block, width), BF16), shape((vocab_rows, width), F32)),
            in_specs=[vmem(), vmem()] + [anywhere()] * 4, out_specs=(vmem(), vmem(), anywhere()),
            scratch_shapes=[VM((tp_size, cols, width), BF16), VM((tp_size, width, cols), BF16), VM((vocab_rows, num_tokens), BF16), VM((num_tokens, width), BF16), VM((vocab_rows, width), F32),
                            VM((block, width), BF16), VM((block, width), BF16), VM((block, tp_size * cols), BF16), DMA((2 * SLOTS,)), DMA((2 * SLOTS,)), DMA((2,)), DMA((5,))],
            compiler_params=params(4), name='backward_chain',
        )(g_top.reshape(block, width), slope, one_t, two_t, g_all, n_all)

        dx_first = spread_call(grad_x, 0, False, 5).reshape(num_tokens, width)

        step = 512
        grad_one, grad_two = pl.pallas_call(
            weight_kernel, grid=(num_tokens // step,),
            out_shape=(shape((width, cols), F32), shape((cols, width), F32)),
            in_specs=[pl.BlockSpec((step, width), lambda i: (i, 0)), pl.BlockSpec((step, width), lambda i: (i, 0)),
                      pl.BlockSpec((width, cols), lambda i: (0, 0)), pl.BlockSpec((cols, width), lambda i: (0, 0))],
            out_specs=(pl.BlockSpec((width, cols), lambda i: (0, 0)), pl.BlockSpec((cols, width), lambda i: (0, 0))),
            compiler_params=pltpu.CompilerParams(vmem_limit_bytes=VMEM_LIMIT), name='weight_grads',
        )(x_all.reshape(num_tokens, width), dy_all.reshape(num_tokens, width), w_one, w_two)

        chain_tok = tok_local.reshape(pp_size, tp_size, unit).transpose(1, 0, 2).reshape(num_tokens)
        one_hot = (chain_tok[:, None] == jnp.arange(vocab_rows, dtype=jnp.int32)[None, :]).astype(BF16)
        grad_table = de_head + contract(one_hot, dx_first, 0, 0)
        return loss.reshape(1) / num_tokens, grad_one[None], grad_two[None], grad_table

    return jax.shard_map(device_fn, mesh=mesh, in_specs=(P('dp', None), P('dp', None), P('tp', None), P('pp', None, 'tp'), P('pp', 'tp', None)), out_specs=(P('dp'), P(('dp', 'pp'), None, 'tp'), P(('dp', 'pp'), 'tp', None), P(('dp', 'tp'), None)), check_vma=False)
```

time: 1110 us -> 378 us (0.34)
  waiting for transfers between devices: 671 us -> 0 us
  Pallas kernels: 0 us -> 348 us
  matrix products: 268 us -> 19.6 us
  starting transfers between devices: 45.8 us -> 0 us
  blocking collectives: 34 us -> 0 us
  other arithmetic: 34.5 us -> 0.74 us
  local copies, waits for them, and re-layouts: 35 us -> 2.47 us
  between operations: 16.9 us -> 2.36 us
    all_gather x6 -> x0, waiting for transfers between devices: 349 us -> none  [the longest x1 78.3 us: device_fn(): w_one_full = lax.all_gather(w_one, 'tp', axis=1, tiled=True)]
    pallas_call x0 -> x6, Pallas kernels: none -> 348 us  [the longest x1 120 us: device_fn(): pl.pallas_call(functools.partial(forward_kernel, last, pp_size // 2), out...]
    dot_general x14 -> x1, matrix products: 189 us -> 19.6 us  [contract(): lax.dot_general(lhs, rhs, (((lhs_dim,), (rhs_dim,)), ((), ())), preferred...]
    reduce_scatter x2 -> x0, waiting for transfers between devices: 146 us -> none  [the longest x1 78.5 us: device_fn(): x_act = lax.psum_scatter(looked, 'tp', scatter_dimension=0, tiled=True)]
    psum x2 -> x0, waiting for transfers between devices: 112 us -> none  [the longest x1 58.4 us: device_fn(): top = lax.psum(jnp.where(is_last, y_act, jnp.zeros_like(y_act)), 'pp')]
    dot_general x10 -> x0, matrix products: 78.3 us -> none  [the longest x8 68.7 us: device_fn(): branch = jnp.dot(gate, w_two_full, preferred_element_type=jnp.float32)]
    ppermute x14 -> x0, waiting for transfers between devices: 61.6 us -> none  [the longest x7 39.4 us: device_fn(): g_act = lax.ppermute(grad_x, 'pp', bwd_perm)]
    ppermute x14 -> x0, starting transfers between devices: 45.4 us -> none  [the longest x7 31.1 us: device_fn(): x_act = lax.ppermute(y_act, 'pp', fwd_perm)]
  transfers between devices with their start and end apart: 24 -> 0, of which waited for: 24 -> 0; matrix products, arithmetic and copies ran while one was open for 2% -> 0% of each run, Pallas kernels for 0% -> 0%
where the time goes in v3:
time: 378 us; the launch traced here: 373 us
  Pallas kernels  348 us (92%)
  matrix products  19.6 us (5%)
    pallas_call x1, Pallas kernels, device_fn(): pl.pallas_call(functools.partial(forward_kernel, last, pp_size // 2), out...  120 us
    pallas_call x2, Pallas kernels, spread_call(): pl.pallas_call(functools.partial(spread_kernel, source, pp_size, head), o...  83.3 us
    pallas_call x1, Pallas kernels, device_fn(): pl.pallas_call(functools.partial(backward_kernel, last, 4, chunk), out_sh...  76.9 us
    pallas_call x1, Pallas kernels, device_fn(): pl.pallas_call(functools.partial(head_kernel, last, pp_size, chunk), out_...  57.9 us
    dot_general x1, matrix products, contract(): lax.dot_general(lhs, rhs, (((lhs_dim,), (rhs_dim,)), ((), ())), preferred...  19.6 us
    pallas_call x1, Pallas kernels, device_fn(): pl.pallas_call(weight_kernel, grid=(num_tokens // step,), out_shape=(shap...  9.49 us

profile of v3, /device:TPU:1, one launch (start us, length us, event | category | flops | bytes accessed | tf_op | source)
XLA Modules:
  0.0 372.8 jit_solution(14668612253357535551)
XLA Ops:
  0.6 0.7 broadcast_subtract_fusion
  1.4 0.7 sub.30.lab_two
  2.1 0.7 sub.29.lab
  2.7 0.1 sub.27
  2.8 0.1 dynamic_slice.3
  2.9 0.1 sub.31
  3.0 0.1 eq.15
  3.1 0.8 copy.9.ids
  3.9 120.1 %forward_chain.1 = (bf16[128,1024]{1,0:T(8,128)(2,1)}, bf16[128,1024]{1,0:T(8,128)(2,1)}, f32[16,128,256]{2,1,0:T(8,128)}, bf16[16,256,1024]{2,1,0:T(8,128)(2,1)}, bf16[16,1024,256]{2,1,0:T(8,128)(2,1)}) custom-call(s32[256,1]{1,0:T(8,128)} %copy.9.ids, bf16[3144,1024]{1,0:T(8,128)(2,1)} %emb.3, bf16[1024,256]{1,0:T(8,128)(2,1)} %bitcast.17, ...), custom_call_target="tpu_custom_call" | custom-call | tf_op jit(solution)/shard_map/forward_chain/pallas_call | solution.py:727
  123.9 51.4 %spread_7.1 = (bf16[16,128,1024]{2,1,0:T(8,128)(2,1)}, bf16[16,1024]{1,0:T(8,128)(2,1)}) custom-call(bf16[128,1024]{1,0:T(8,128)(2,1)} %get-tuple-element.21.y_ref), custom_call_target="tpu_custom_call" | custom-call | tf_op jit(solution)/shard_map/spread_7/pallas_call | solution.py:743
  175.4 57.9 %head.1 = (f32[1,1]{1,0:T(1,128)}, bf16[3144,2048]{1,0:T(8,128)(2,1)}, bf16[2048,1024]{1,0:T(8,128)(2,1)}, bf16[8,16,1024]{2,1,0:T(8,128)(2,1)}, bf16[16,128,1024]{2,1,0:T(8,128)(2,1)}) custom-call(bf16[3144,1024]{1,0:T(8,128)(2,1)} %emb.3, bf16[16,128,1024]{2,1,0:T(8,128)(2,1)} %get-tuple-element.22.top, s32[8,256]{1,0:T(8,128)} %sub.29.lab, ...), custom_call_target="tpu_custom_call" | custom-call | tf_op jit(solution)/shard_map/head/pallas_call | solution.py:752
  233.8 76.9 %backward_chain.1 = (bf16[128,1024]{1,0:T(8,128)(2,1)}, bf16[16,128,1024]{2,1,0:T(8,128)(2,1)}, f32[3144,1024]{1,0:T(8,128)}) custom-call(bf16[128,1024]{1,0:T(8,128)(2,1)} %bitcast.21, f32[16,128,256]{2,1,0:T(8,128)} %get-tuple-element.28.slope_ref, bf16[16,256,1024]{2,1,0:T(8,128)(2,1)} %get-tuple-element.29.one_all, ...), custom_call_target="tpu_custom_call" | custom-call | tf_op jit(solution)/shard_map/backward_chain/pallas_call | solution.py:763
  310.7 9.5 %weight_grads.1 = (f32[1024,256]{1,0:T(8,128)}, f32[256,1024]{1,0:T(8,128)}) custom-call(bf16[2048,1024]{1,0:T(8,128)(2,1)} %bitcast.14, bf16[2048,1024]{1,0:T(8,128)(2,1)} %bitcast.15, bf16[1024,256]{1,0:T(8,128)(2,1)} %bitcast.18, bf16[256,1024]{1,0:T(8,128)(2,1)} %bitcast.20), custom_call_target="tpu_custom_call" | custom-call | tf_op jit(solution)/shard_map/weight_grads/pallas_call | solution.py:775
  320.2 31.9 %spread_0.1 = bf16[16,128,1024]{2,1,0:T(8,128)(2,1)} custom-call(bf16[128,1024]{1,0:T(8,128)(2,1)} %get-tuple-element.37.y_ref), custom_call_target="tpu_custom_call" | custom-call | tf_op jit(solution)/shard_map/spread_0/pallas_call | solution.py:743
  352.1 19.6 %fusion.2 = f32[3144,1024]{1,0:T(8,128)} fusion(f32[3144,1024]{1,0:T(8,128)} %get-tuple-element.36, bf16[2048,1024]{1,0:T(8,128)(2,1)} %bitcast.16, s32[2048]{0:T(1024)S(1)} %eq.15), kind=kOutput, calls=%fused_computation.3 | convolution fusion | flops 13196550144 | bytes 29958144 | tf_op jit(solution)/shard_map/dot_general | solution.py:21
  (1 shorter events, 0.0 us)
